TPU v7x, 32 devices: a whole 2x2x4 slice. The times are simulated.
32 devices in a mesh: cells: 16 (over z, y, x), faces: 2 (over core).
Axes of the slice: x: 2, y: 2, z: 4, core: 2. Of those that a mesh axis runs over, the one named last changes fastest.
Arguments:
- flow_state: float32 [4, 131072], P(None, 'cells'), may hold values from -6 to 6
- source_term: float32 [4, 131072], P(None, 'cells'), may hold values from -24 to 24
- volume_rate: float32 [131072], P('cells'), may hold values from 0.5 to 4
- face_normal: float32 [3, 393216], P(None, ('cells', 'faces')), may hold values from -3 to 3
- face_owner: int32 [393216], P(('cells', 'faces')), may hold values from 0 to 8191, as said below
- face_neighbour: int32 [393216], P(('cells', 'faces')), may hold values from 0 to 9727, as said below
- face_count: int32 [32], P(('cells', 'faces')), may hold values from 1536 to 12288, as said below
- send_list: int32 [96, 256], P('cells'), may hold values from 0 to 8191
- halo_count: int32 [96], P('cells'), may hold values from 64 to 256, as said below
Outputs:
- solution_field: float32 [4, 131072], P(None, 'cells')
- residual: float32 [4, 131072], P(None, 'cells')
Inputs may be any that keep to these rules, and one draw needn't show every extreme that they name: `face_owner`: A local cell of the slot's partition; with s = g mod 12288 and t = s // 192, it lies in 128 * t to 128 * t + 127. `face_neighbour`: with s and t as for face_owner: below 8192 a local cell (128 * t + d) mod 8192 with d in 0 to 255; otherwise 8192 plus a halo slot of the slot's partition in (t mod (6)) * 256 to that plus 256 - 1. Live slots of a block are its first face_count slots; in every draw some block has all 12288 slots live. `send_list`: entries at or past the list's count are unused. `halo_count`: every partition has one list with exactly 256 entries.
All inputs are finite; a program needn't handle non-finite values.
Results may differ from a plain program's by a relative error of at most 0.0003.
Values sent between devices are 32-bit elements; how exact they have to be, the bound alone decides.
A program may use at most 64 MiB of HBM per device.

v0:
```python
import functools

import jax
import jax.numpy as jnp
from jax import lax
from jax.experimental import pallas as pl
from jax.experimental.pallas import tpu as pltpu
from jax.sharding import PartitionSpec as P

ITERS = 2
LANES = 128
MESH = pl.DeviceIdType.MESH
F32 = jnp.float32
BF16 = jnp.bfloat16


def take_lanes(source, index):
    return jnp.take_along_axis(source, index, axis=1, mode="promise_in_bounds")


def split(value):
    high = value.astype(BF16).astype(F32)
    return high, value - high


def kernel(
    parts,
    cores,
    count_ref,
    flow_hbm,
    source_hbm,
    volume_hbm,
    normal_hbm,
    owner_hbm,
    neighbour_hbm,
    list_ref,
    halo_count_ref,
    solution_ref,
    residual_ref,
    flow_ref,
    source_ref,
    volume_ref,
    normal_ref,
    owner_ref,
    neighbour_ref,
    input_sem,
    own_lane,
    right_lane,
    right_kind,
    own_row,
    local_row,
    face_u,
    face_s,
    face_n,
    signed_hot,
    plain_hot,
    flux_rows,
    size_rows,
    cell_rows,
    size_cells,
    fields,
    halo_rows,
    blocks,
    vecs,
    pair_out,
    pair_in,
    halo_out,
    halo_in,
    dot_out,
    dot_in,
    pair_send,
    pair_recv,
    halo_send,
    halo_recv,
    dot_send,
    dot_recv,
):
    me = lax.axis_index("cells")
    core = lax.axis_index("faces")
    other = (core + 1) % cores
    tiles = volume_ref.shape[0]
    pairs = tiles // 2
    groups = pairs // 8
    cells = tiles * LANES
    lists = halo_in.shape[1]
    lists_here = lists // cores
    width = list_ref.shape[1] * LANES

    def fetched(number, source, target):
        copy = pltpu.make_async_copy(source, target, input_sem.at[number])
        copy.start()
        return copy

    copies = [
        fetched(0, owner_hbm, owner_ref),
        fetched(1, neighbour_hbm, neighbour_ref),
        fetched(2, flow_hbm, flow_ref),
        fetched(4, source_hbm, source_ref),
        fetched(5, volume_hbm, volume_ref),
    ]
    normals = [fetched(3, normal_hbm, normal_ref.at[pl.ds(0, 3 * pairs)])]

    barrier = pltpu.get_barrier_semaphore()
    for step in range(1, parts * cores):
        number = (me * cores + core + step) % (parts * cores)
        pl.semaphore_signal(
            barrier,
            inc=1,
            device_id={"cells": number // cores, "faces": number % cores},
            device_id_type=MESH,
        )

    lane = lax.broadcasted_iota(jnp.int32, (pairs, LANES), 1)
    pair_id = lax.broadcasted_iota(jnp.int32, (pairs, LANES), 0)
    late = lane >= LANES // 2
    count = count_ref[0]
    for copy in copies:
        copy.wait()
    for j in range(3):
        tile = 2 * pair_id + (0 if j == 0 else 1)
        if j == 1:
            tile = 2 * pair_id + late.astype(jnp.int32)
        owner = owner_ref[pl.ds(j, pairs, stride=3), :]
        beside = neighbour_ref[pl.ds(j, pairs, stride=3), :]
        live = (3 * pair_id + j) * LANES + lane < count
        is_local = beside < cells
        column = beside - tile * LANES
        column = jnp.where(column < 0, column + cells, column)
        slot = beside - cells - (tile % lists) * width
        place = jnp.where(is_local, column, slot)
        upper = place >= LANES
        own = owner - tile * LANES
        own_lane[j] = own
        right_lane[j] = jnp.where(upper, place - LANES, place)
        right_kind[j] = jnp.where(is_local, 0, 2) + upper.astype(jnp.int32)
        own_row[j] = jnp.where(live, own, -1).astype(F32)
        local_row[j] = jnp.where(live & is_local, column, -1).astype(F32)

    def start_halo(turn, field):
        row8 = lax.broadcasted_iota(jnp.int32, (8, LANES), 0)
        for i in range(lists_here):
            which = core * lists_here + i
            rows = []
            wanted = list_ref[which]
            limit = halo_count_ref[which]
            for b in range(4):
                for half in range(2):
                    cell = jnp.broadcast_to(wanted[half : half + 1], (8, LANES))
                    row = cell // LANES
                    col = cell - row * LANES
                    found = jnp.zeros((8, LANES), F32)
                    for g in range(tiles // 8):
                        got = take_lanes(field(b, g), col)
                        found = jnp.where(row == row8 + 8 * g, got, found)
                    found = jnp.sum(found, axis=0, keepdims=True)
                    used = (
                        lax.broadcasted_iota(jnp.int32, (1, LANES), 1) + half * LANES < limit
                    )
                    rows.append(jnp.where(used, found, 0.0))
            halo_out[turn, i] = jnp.concatenate(rows, axis=0)
        for i in range(lists_here):
            target = (me + (1 - 2 * core) * (i + 1) + parts) % parts
            for c in range(cores):
                pltpu.make_async_remote_copy(
                    src_ref=halo_out.at[turn, i],
                    dst_ref=halo_in.at[turn, core * lists_here + i],
                    send_sem=halo_send.at[turn],
                    recv_sem=halo_recv.at[turn],
                    device_id={"cells": target, "faces": c},
                    device_id_type=MESH,
                ).start()

    def wait_halo(turn):
        pltpu.make_async_copy(halo_in.at[turn], halo_in.at[turn], halo_recv.at[turn]).wait()
        return [halo_in[turn, k] for k in range(lists)]

    def start_pair(turn, rows):
        copy = pltpu.make_async_remote_copy(
            src_ref=pair_out.at[turn, pl.ds(0, rows)],
            dst_ref=pair_in.at[turn, pl.ds(0, rows)],
            send_sem=pair_send.at[turn],
            recv_sem=pair_recv.at[turn],
            device_id={"cells": me, "faces": other},
            device_id_type=MESH,
        )
        copy.start()
        return copy

    def start_dots(turn, partials):
        at = lax.broadcasted_iota(jnp.int32, (1, LANES), 1)
        packed = jnp.zeros((1, LANES), F32)
        for d, p in enumerate(partials):
            row = jnp.sum(p.reshape(tiles // 8, 8, LANES).sum(axis=0), axis=0, keepdims=True)
            packed = jnp.where(at == d, jnp.sum(row, axis=1, keepdims=True), packed)
        dot_out[turn] = packed
        dot_in[turn, me] = packed
        for step in range(1, parts):
            pltpu.make_async_remote_copy(
                src_ref=dot_out.at[turn],
                dst_ref=dot_in.at[turn, me],
                send_sem=dot_send.at[turn],
                recv_sem=dot_recv.at[turn],
                device_id={"cells": (me + step) % parts, "faces": core},
                device_id_type=MESH,
            ).start()

    def wait_dots(turn, number):
        part = dot_in.at[turn, pl.ds(0, parts - 1)]
        pltpu.make_async_copy(part, part, dot_recv.at[turn]).wait()
        total = dot_in[turn, 0]
        for q in range(1, parts):
            total = total + dot_in[turn, q]
        return [jnp.broadcast_to(total[:, d : d + 1], (1, LANES)) for d in range(number)]

    def put_field(values, halos):
        for b, value in enumerate(values):
            fields[b, pl.ds(0, tiles), :] = value
            fields[b, pl.ds(tiles, 1), :] = value[0:1]
        period = halo_rows.shape[0] // 8
        for t in range(period):
            halo_rows[pl.ds(t, 8, stride=period), :] = halos[t % lists]

    def sides(g, j, b):
        period = halo_rows.shape[0] // 8
        here = pl.multiple_of(g * 8, 8)
        left_at = own_lane[j, pl.ds(here, 8), :]
        right_at = right_lane[j, pl.ds(here, 8), :]
        kind = right_kind[j, pl.ds(here, 8), :]

        def of_tile(odd):
            first = 16 * g + odd
            halo_first = (16 * g) % lists + odd
            low = fields[b, pl.ds(first, 8, stride=2), :]
            high = fields[b, pl.ds(first + 1, 8, stride=2), :]
            halo_low = halo_rows[pl.ds(2 * b * period + halo_first, 8, stride=2), :]
            halo_high = halo_rows[pl.ds((2 * b + 1) * period + halo_first, 8, stride=2), :]
            left = take_lanes(low, left_at)
            right = jnp.where(
                kind < 2,
                jnp.where(kind == 0, take_lanes(low, right_at), take_lanes(high, right_at)),
                jnp.where(
                    kind == 2, take_lanes(halo_low, right_at), take_lanes(halo_high, right_at)
                ),
            )
            return left, right

        if j == 0:
            return of_tile(0)
        if j == 2:
            return of_tile(1)
        early = lax.broadcasted_iota(jnp.int32, (8, LANES), 1) < LANES // 2
        left_a, right_a = of_tile(0)
        left_b, right_b = of_tile(1)
        return jnp.where(early, left_a, left_b), jnp.where(early, right_a, right_b)

    def put_flux(ref, g, j, b, value):
        high, low = split(value)
        ref[j, pl.ds(64 * g + b, 8, stride=8), :] = high
        ref[j, pl.ds(64 * g + 4 + b, 8, stride=8), :] = low

    def tile_rows(rows_ref, u, odd):
        at = pl.ds(pl.multiple_of(u * 8, 8), 8)
        return jnp.concatenate([rows_ref[odd, at, :], rows_ref[odd + 1, at, :]], axis=1).astype(BF16)

    def added(rows, hot):
        return lax.dot_general(
            rows, hot, (((1,), (1,)), ((), ())), preferred_element_type=F32
        )

    def scatter(u):
        for odd in range(2):
            result = added(tile_rows(flux_rows, u, odd), signed_hot[2 * u + odd])
            at = pl.ds(pl.multiple_of(u * 16 + odd * 8, 8), 8)
            cell_rows[0, at, :] = result[:, :LANES]
            cell_rows[1, at, :] = result[:, LANES:]

    def scatter_size(u):
        for odd in range(2):
            rows = tile_rows(size_rows, u, odd)
            at = pl.ds(pl.multiple_of(u * 16 + odd * 8, 8), 8)
            size_cells[0, at, :] = added(rows, plain_hot[2 * u + odd])
            size_cells[1, at, :] = -added(rows, signed_hot[2 * u + odd, LANES:, :])

    def collect(cells_ref, b):
        def rows(first, side):
            return cells_ref[side, pl.ds(first, tiles, stride=8), :]

        low = rows(b, 0) + rows(4 + b, 0)
        high = rows(b, 1) + rows(4 + b, 1)
        high = jnp.concatenate([high[tiles - 1 :], high[: tiles - 1]], axis=0)
        return low + high

    def apply_matrix(turn, values, halos):
        put_field(values, halos)

        def group(g, carry):
            here = pl.multiple_of(g * 8, 8)
            for j in range(3):
                u = face_u[j, pl.ds(here, 8), :]
                s = face_s[j, pl.ds(here, 8), :]
                n = [face_n[i, j, pl.ds(here, 8), :] for i in range(3)]
                both = [sides(g, j, b) for b in range(4)]
                total = [left + right for left, right in both]
                jump = [s * (right - left) for left, right in both]
                for i in range(3):
                    put_flux(flux_rows, g, j, i, u * total[i] + n[i] * total[3] - jump[i])
                last = n[0] * total[0] + n[1] * total[1] + n[2] * total[2] - jump[3]
                put_flux(flux_rows, g, j, 3, last)
            for i in range(8):
                scatter(g * 8 + i)
            return carry

        lax.fori_loop(0, groups, group, 0)
        mine = [collect(cell_rows, b) for b in range(4)]
        for b in range(4):
            pair_out[turn, b * tiles : (b + 1) * tiles, :] = mine[b]
        copy = start_pair(turn, 4 * tiles)
        copy.wait_recv()
        volume = volume_ref[...]
        return [
            volume * values[b]
            + (
                pair_out[turn, b * tiles : (b + 1) * tiles, :]
                + pair_in[turn, b * tiles : (b + 1) * tiles, :]
            )
            for b in range(4)
        ]

    def precondition(w):
        rvd, rschur = blocks[0], blocks[1]
        n = [blocks[2 + i] for i in range(3)]
        pressure = (w[3] - (n[0] * w[0] + n[1] * w[1] + n[2] * w[2]) * rvd) * rschur
        return [(w[i] - n[i] * pressure) * rvd for i in range(3)] + [pressure]

    def load(which):
        return [vecs[which, b] for b in range(4)]

    def save(which, values):
        for b in range(4):
            vecs[which, b] = values[b]

    def dot(a, b):
        return a[0] * b[0] + a[1] * b[1] + a[2] * b[2] + a[3] * b[3]

    def saved_field(which):
        return lambda b, g: vecs[which, b, 8 * g : 8 * g + 8, :]

    PRE, IMAGE_M, TEMP = 0, 1, 2
    flow = [flow_ref[pl.ds(b, tiles, stride=4), :] for b in range(4)]
    source = [source_ref[pl.ds(b, tiles, stride=4), :] for b in range(4)]
    pl.semaphore_wait(barrier, parts * cores - 1)
    start_halo(0, lambda b, g: flow_ref[pl.ds(32 * g + b, 8, stride=4), :])
    start_dots(0, [dot(source, source)])

    cell_id = lax.broadcasted_iota(jnp.int32, (LANES, LANES), 0).astype(F32).astype(BF16)
    early_row = lax.broadcasted_iota(jnp.int32, (1, LANES), 1) < LANES // 2
    one, zero = jnp.ones((), BF16), jnp.zeros((), BF16)

    def hot_of(row):
        return jnp.where(cell_id == row.astype(BF16), one, zero)

    def build(u, carry):
        for odd in range(2):
            for half in range(2):
                j = odd + half
                own = own_row[j, pl.ds(u, 1), :]
                local = local_row[j, pl.ds(u, 1), :]
                if j == 1:
                    keep = early_row if odd == 0 else jnp.logical_not(early_row)
                    own = jnp.where(keep, own, -1.0)
                    local = jnp.where(keep, local, -1.0)
                own_hot, local_hot = hot_of(own), hot_of(local)
                lanes = slice(half * LANES, (half + 1) * LANES)
                signed_hot[2 * u + odd, :LANES, lanes] = own_hot - local_hot
                signed_hot[2 * u + odd, LANES:, lanes] = -hot_of(local - LANES)
                plain_hot[2 * u + odd, :, lanes] = own_hot + local_hot
        return carry

    lax.fori_loop(0, pairs, build, 0)
    size_rows[...] = jnp.zeros_like(size_rows)
    for copy in normals:
        copy.wait()

    put_field(flow, wait_halo(0))

    def face_terms(g, carry):
        here = pl.multiple_of(g * 8, 8)
        for j in range(3):
            n = [normal_ref[pl.ds(24 * g + j, 8, stride=3), i, :] for i in range(3)]
            both = [sides(g, j, b) for b in range(3)]
            total = [left + right for left, right in both]
            u = 0.5 * (n[0] * total[0] + n[1] * total[1] + n[2] * total[2])
            s = jnp.abs(u) + 2.0 * jnp.sqrt(n[0] * n[0] + n[1] * n[1] + n[2] * n[2])
            u, s = 0.5 * u, 0.5 * s
            n = [0.5 * n[i] for i in range(3)]
            face_u[j, pl.ds(here, 8), :] = u
            face_s[j, pl.ds(here, 8), :] = s
            put_flux(flux_rows, g, j, 0, u)
            for i in range(3):
                face_n[i, j, pl.ds(here, 8), :] = n[i]
                put_flux(flux_rows, g, j, 1 + i, n[i])
            put_flux(size_rows, g, j, 0, s)
        for i in range(8):
            scatter(g * 8 + i)
            scatter_size(g * 8 + i)
        return carry

    lax.fori_loop(0, groups, face_terms, 0)
    for b in range(4):
        pair_out[0, b * tiles : (b + 1) * tiles, :] = collect(cell_rows, b)
    pair_out[0, 4 * tiles : 5 * tiles, :] = collect(size_cells, 0)
    start_pair(0, 5 * tiles).wait_recv()
    sums = [
        pair_out[0, b * tiles : (b + 1) * tiles, :] + pair_in[0, b * tiles : (b + 1) * tiles, :]
        for b in range(5)
    ]
    volume = volume_ref[...]
    rvd = 1.0 / (volume + sums[0] + sums[4])
    coupling = sums[1:4]
    norm = coupling[0] * coupling[0] + coupling[1] * coupling[1] + coupling[2] * coupling[2]
    blocks[0] = rvd
    blocks[1] = 1.0 / (volume + sums[4] - norm * rvd)
    for i in range(3):
        blocks[2 + i] = coupling[i]

    def combine(a, scale, b):
        return [x + scale * y for x, y in zip(a, b)]

    residual = source
    direction = source
    pre_dir = precondition(direction)
    save(PRE, pre_dir)
    start_halo(1, saved_field(PRE))
    (rho,) = wait_dots(0, 1)
    halo_dir = wait_halo(1)
    halo_res = halo_dir
    answer = None
    for iteration in range(ITERS):
        final = iteration + 1 == ITERS
        turn = 1 + 2 * iteration
        image = apply_matrix(turn, pre_dir, halo_dir)
        start_dots(turn, [dot(source, image)])
        pre_image = precondition(image)
        save(IMAGE_M, pre_image)
        start_halo(turn + 1, saved_field(IMAGE_M))
        pre_res = pre_dir if iteration == 0 else precondition(residual)
        (shadow_image,) = wait_dots(turn, 1)
        alpha = rho / shadow_image
        middle = combine(residual, -alpha, image)
        pre_mid = combine(pre_res, -alpha, pre_image)
        halo_image = wait_halo(turn + 1)
        halo_mid = combine(halo_res, -alpha, halo_image)
        second = apply_matrix(turn + 1, pre_mid, halo_mid)
        start_dots(
            turn + 1,
            [dot(second, middle), dot(second, second), dot(source, middle), dot(source, second)],
        )
        if not final:
            pre_second = precondition(second)
            save(TEMP, pre_second)
            start_halo(turn + 2, saved_field(TEMP))
        second_mid, second_sq, shadow_mid, shadow_second = wait_dots(turn + 1, 4)
        omega = second_mid / second_sq
        step = combine([alpha * v for v in pre_dir], omega, pre_mid)
        answer = step if answer is None else [a + s for a, s in zip(answer, step)]
        residual = combine(middle, -omega, second)
        if not final:
            rho_next = shadow_mid - omega * shadow_second
            beta = rho_next / rho * (alpha / omega)
            rho = rho_next
            direction = combine(residual, beta, combine(direction, -omega, image))
            pre_dir = precondition(direction)
            halo_second = wait_halo(turn + 2)
            halo_res = combine(halo_mid, -omega, halo_second)
            halo_dir = combine(halo_res, beta, combine(halo_dir, -omega, halo_image))
    for b in range(4):
        solution_ref[pl.ds(b, tiles, stride=4), :] = answer[b]
        residual_ref[pl.ds(b, tiles, stride=4), :] = residual[b]

    for turn in range(halo_in.shape[0]):
        pltpu.make_async_copy(halo_in.at[turn], halo_in.at[turn], halo_send.at[turn]).wait()
    for turn in range(pair_in.shape[0]):
        part = pair_out.at[turn, pl.ds(0, (5 if turn == 0 else 4) * tiles)]
        pltpu.make_async_copy(part, part, pair_send.at[turn]).wait()
        part = dot_in.at[turn, pl.ds(0, parts - 1)]
        pltpu.make_async_copy(part, part, dot_send.at[turn]).wait()


def body(
    flow_state,
    source_term,
    volume_rate,
    face_normal,
    face_owner,
    face_neighbour,
    face_count,
    send_list,
    halo_count,
):
    parts = lax.axis_size("cells")
    cores = lax.axis_size("faces")
    cells = flow_state.shape[1]
    tiles = cells // LANES
    pairs = tiles // 2
    face_rows = face_owner.shape[0] // LANES
    lists, width = send_list.shape
    period = -(-(lists + 16) // 8) * 8
    turns = 1 + 2 * ITERS

    def by_tile(field):
        return field.reshape(4, tiles, LANES).transpose(1, 0, 2).reshape(4 * tiles, LANES)

    def by_component(field):
        return field.reshape(tiles, 4, LANES).transpose(1, 0, 2).reshape(4, cells)

    vmem = pl.BlockSpec(memory_space=pltpu.VMEM)
    hbm = pl.BlockSpec(memory_space=pl.ANY)
    smem = pl.BlockSpec(memory_space=pltpu.SMEM)
    ints = pltpu.VMEM((3, pairs, LANES), jnp.int32)
    floats = pltpu.VMEM((3, pairs, LANES), F32)
    hot = pltpu.VMEM((tiles, 2 * LANES, 2 * LANES), BF16)
    out = jax.ShapeDtypeStruct((4 * tiles, LANES), F32)
    solved, left = pl.pallas_call(
        functools.partial(kernel, parts, cores),
        out_shape=(out, out),
        in_specs=[smem] + [hbm] * 6 + [vmem, smem],
        out_specs=(vmem, vmem),
        scratch_shapes=[
            pltpu.VMEM((4 * tiles, LANES), F32),
            pltpu.VMEM((4 * tiles, LANES), F32),
            pltpu.VMEM((tiles, LANES), F32),
            pltpu.VMEM((face_rows + 8, 3, LANES), F32),
            pltpu.VMEM((face_rows, LANES), jnp.int32),
            pltpu.VMEM((face_rows, LANES), jnp.int32),
            pltpu.SemaphoreType.DMA((6,)),
            ints,
            ints,
            ints,
            floats,
            floats,
            floats,
            floats,
            pltpu.VMEM((3, 3, pairs, LANES), F32),
            hot,
            pltpu.VMEM((tiles, LANES, 2 * LANES), BF16),
            pltpu.VMEM((3, 8 * pairs, LANES), F32),
            pltpu.VMEM((3, 8 * pairs, LANES), F32),
            pltpu.VMEM((2, 8 * tiles, LANES), F32),
            pltpu.VMEM((2, 8 * tiles, LANES), F32),
            pltpu.VMEM((4, tiles + 8, LANES), F32),
            pltpu.VMEM((8 * period, LANES), F32),
            pltpu.VMEM((5, tiles, LANES), F32),
            pltpu.VMEM((3, 4, tiles, LANES), F32),
            pltpu.VMEM((turns, 5 * tiles, LANES), F32),
            pltpu.VMEM((turns, 5 * tiles, LANES), F32),
            pltpu.VMEM((turns, lists // cores, 8, LANES), F32),
            pltpu.VMEM((turns, lists, 8, LANES), F32),
            pltpu.VMEM((turns + 8, 1, LANES), F32),
            pltpu.VMEM((turns, parts + 8, 1, LANES), F32),
        ]
        + [pltpu.SemaphoreType.DMA((turns,))] * 6,
        compiler_params=pltpu.CompilerParams(
            collective_id=0, has_side_effects=True, vmem_limit_bytes=56 * 1024 * 1024
        ),
    )(
        face_count,
        by_tile(flow_state),
        by_tile(source_term),
        volume_rate.reshape(tiles, LANES),
        face_normal.reshape(3, face_rows, LANES).transpose(1, 0, 2),
        face_owner.reshape(face_rows, LANES),
        face_neighbour.reshape(face_rows, LANES),
        send_list.reshape(lists, width // LANES, LANES),
        halo_count,
    )
    return by_component(solved), by_component(left)


def solution(mesh):
    in_specs = (
        P(None, "cells"),
        P(None, "cells"),
        P("cells"),
        P(None, ("cells", "faces")),
        P(("cells", "faces")),
        P(("cells", "faces")),
        P(("cells", "faces")),
        P("cells", None),
        P("cells"),
    )
    out_specs = (P(None, "cells"), P(None, "cells"))
    return jax.shard_map(body, mesh=mesh, in_specs=in_specs, out_specs=out_specs, check_vma=False)
```

profile of v0, /device:TPU:0, one launch (start us, length us, event | category | flops | bytes accessed | tf_op | source)
XLA Modules:
  0.0 64.4 jit_solution(3804672061715814383)
XLA Ops:
  0.6 0.0 copy-start.1
  1.3 0.0 copy-done.1
  1.3 0.6 reshape.51.list_ref
  1.9 60.2 %shard_map.104 = (f32[256,128]{1,0:T(8,128)}, f32[256,128]{1,0:T(8,128)}) custom-call(s32[1]{0:T(128)S(6)} %copy.17.count_ref, f32[256,128]{1,0:T(8,128)} %bitcast.29, f32[256,128]{1,0:T(8,128)} %bitcast.30, f32[64,128]{1,0:T(8,128)} %bitcast.33, f32[96,3,128]{2,1,0:T(4,128)} %bitcast.26, s32[96,128]{1,0:T(8,128)} %bitcast.31, s32[96,128]{1,0:T(8,128)} %bitcast.32, ...), custom_call_target="tpu_custom_call" | custom-call | tf_op jit(solution)/shard_map/pallas_call | solution.py:523
  62.1 0.0 copy-start
  62.2 1.6 %copy.18 = f32[4,8192]{1,0:T(4,128)} copy(f32[4,8192]{1,0:T(4,128)} %bitcast.28) | data formatting | bytes 262144
  63.8 0.0 copy-done
  63.8 0.7 %copy.19 = f32[4,8192]{1,0:T(4,128)} copy(f32[4,8192]{1,0:T(4,128)S(1)} %bitcast.27) | data formatting | bytes 262144
Async XLA Ops:
  0.6 0.7 %copy-start.1 = (s32[6,256]{1,0:T(8,128)S(1)}, s32[6,256]{1,0:T(8,128)}, u32[]{:S(2)}) copy-start(s32[6,256]{1,0:T(8,128)} %param.16) | copy-start | bytes 18436
  62.1 1.6 %copy-start = (f32[256,128]{1,0:T(8,128)S(1)}, f32[256,128]{1,0:T(8,128)}, u32[]{:S(2)}) copy-start(f32[256,128]{1,0:T(8,128)} %get-tuple-element.5) | copy-start | bytes 393220
where the time goes:
time: 64.7 us; the launch traced here: 64.4 us
  Pallas kernels  60.2 us (93%)
  local copies, waits for them, and re-layouts  2.9 us (4%)
  between operations  1.31 us (2%)
    pallas_call x1, Pallas kernels, body(): pl.pallas_call(functools.partial(kernel, parts, cores), out_shape=(out, o...  60.2 us
    unnamed x6, local copies, waits for them, and re-layouts  2.29 us

commit v1 on v0

--- a/solution.py
+++ b/solution.py
@@ -260,11 +260,15 @@
 
     def tile_rows(rows_ref, u, odd):
         at = pl.ds(pl.multiple_of(u * 8, 8), 8)
-        return jnp.concatenate([rows_ref[odd, at, :], rows_ref[odd + 1, at, :]], axis=1).astype(BF16)
+        middle = rows_ref[1, at, :]
+        if odd:
+            middle = pltpu.roll(middle, LANES // 2, 1)
+        rows = jnp.concatenate([rows_ref[2 * odd, at, :], middle], axis=1)
+        return rows[:, : 3 * LANES // 2]
 
     def added(rows, hot):
         return lax.dot_general(
-            rows, hot, (((1,), (1,)), ((), ())), preferred_element_type=F32
+            rows.astype(BF16), hot, (((1,), (0,)), ((), ())), preferred_element_type=F32
         )
 
     def scatter(u):
@@ -276,10 +280,14 @@
 
     def scatter_size(u):
         for odd in range(2):
-            rows = tile_rows(size_rows, u, odd)
+            sizes = tile_rows(size_rows, u, odd)
+            rows = jnp.concatenate([tile_rows(flux_rows, u, odd), sizes], axis=0)
             at = pl.ds(pl.multiple_of(u * 16 + odd * 8, 8), 8)
-            size_cells[0, at, :] = added(rows, plain_hot[2 * u + odd])
-            size_cells[1, at, :] = -added(rows, signed_hot[2 * u + odd, LANES:, :])
+            result = added(rows, signed_hot[2 * u + odd])
+            cell_rows[0, at, :] = result[:8, :LANES]
+            cell_rows[1, at, :] = result[:8, LANES:]
+            size_cells[0, at, :] = added(sizes, plain_hot[2 * u + odd])
+            size_cells[1, at, :] = -result[8:, LANES:]
 
     def collect(cells_ref, b):
         def rows(first, side):
@@ -352,31 +360,40 @@
     start_halo(0, lambda b, g: flow_ref[pl.ds(32 * g + b, 8, stride=4), :])
     start_dots(0, [dot(source, source)])
 
-    cell_id = lax.broadcasted_iota(jnp.int32, (LANES, LANES), 0).astype(F32).astype(BF16)
-    early_row = lax.broadcasted_iota(jnp.int32, (1, LANES), 1) < LANES // 2
+    cell_id = lax.broadcasted_iota(jnp.int32, (LANES, LANES), 1).astype(F32).astype(BF16)
     one, zero = jnp.ones((), BF16), jnp.zeros((), BF16)
 
-    def hot_of(row):
-        return jnp.where(cell_id == row.astype(BF16), one, zero)
-
-    def build(u, carry):
-        for odd in range(2):
-            for half in range(2):
-                j = odd + half
-                own = own_row[j, pl.ds(u, 1), :]
-                local = local_row[j, pl.ds(u, 1), :]
-                if j == 1:
-                    keep = early_row if odd == 0 else jnp.logical_not(early_row)
-                    own = jnp.where(keep, own, -1.0)
-                    local = jnp.where(keep, local, -1.0)
-                own_hot, local_hot = hot_of(own), hot_of(local)
-                lanes = slice(half * LANES, (half + 1) * LANES)
-                signed_hot[2 * u + odd, :LANES, lanes] = own_hot - local_hot
-                signed_hot[2 * u + odd, LANES:, lanes] = -hot_of(local - LANES)
-                plain_hot[2 * u + odd, :, lanes] = own_hot + local_hot
-        return carry
-
-    lax.fori_loop(0, pairs, build, 0)
+    def by_face(rows):
+        flat = rows[...].reshape(3 * pairs, LANES)
+        spare = -(3 * pairs) % LANES
+        flat = jnp.concatenate([flat, jnp.zeros((spare, LANES), F32)], axis=0)
+        return flat.T.astype(BF16)
+
+    own_faces, local_faces = by_face(own_row), by_face(local_row)
+
+    def hot_of(column):
+        return jnp.where(cell_id == column, one, zero)
+
+    for u in range(pairs):
+        for j in range(3):
+            at = j * pairs + u
+            own = jnp.broadcast_to(own_faces[:, at : at + 1], (LANES, LANES))
+            local = jnp.broadcast_to(local_faces[:, at : at + 1], (LANES, LANES))
+            own_hot, local_hot = hot_of(own), hot_of(local)
+            low = own_hot - local_hot
+            high = -hot_of(local - LANES)
+            plain = own_hot + local_hot
+            half = LANES // 2
+            if j == 1:
+                places = [(2 * u, LANES, 0, half), (2 * u + 1, LANES, half, LANES)]
+            else:
+                places = [(2 * u + j // 2, 0, 0, LANES)]
+            for tile, row, first, last in places:
+                rows = slice(row, row + last - first)
+                signed_hot[tile, rows, :LANES] = low[first:last]
+                signed_hot[tile, rows, LANES:] = high[first:last]
+                plain_hot[tile, rows, :] = plain[first:last]
+
     size_rows[...] = jnp.zeros_like(size_rows)
     for copy in normals:
         copy.wait()
@@ -401,7 +418,6 @@
                 put_flux(flux_rows, g, j, 1 + i, n[i])
             put_flux(size_rows, g, j, 0, s)
         for i in range(8):
-            scatter(g * 8 + i)
             scatter_size(g * 8 + i)
         return carry
 
@@ -518,7 +534,7 @@
     smem = pl.BlockSpec(memory_space=pltpu.SMEM)
     ints = pltpu.VMEM((3, pairs, LANES), jnp.int32)
     floats = pltpu.VMEM((3, pairs, LANES), F32)
-    hot = pltpu.VMEM((tiles, 2 * LANES, 2 * LANES), BF16)
+    hot = pltpu.VMEM((tiles, 3 * LANES // 2, 2 * LANES), BF16)
     out = jax.ShapeDtypeStruct((4 * tiles, LANES), F32)
     solved, left = pl.pallas_call(
         functools.partial(kernel, parts, cores),
@@ -542,7 +558,7 @@
             floats,
             pltpu.VMEM((3, 3, pairs, LANES), F32),
             hot,
-            pltpu.VMEM((tiles, LANES, 2 * LANES), BF16),
+            pltpu.VMEM((tiles, 3 * LANES // 2, LANES), BF16),
             pltpu.VMEM((3, 8 * pairs, LANES), F32),
             pltpu.VMEM((3, 8 * pairs, LANES), F32),
             pltpu.VMEM((2, 8 * tiles, LANES), F32),

time: 64.7 us -> 57.2 us (0.88)
  Pallas kernels: 60.2 us -> 52.7 us
    pallas_call x1, Pallas kernels: 60.2 us -> 52.7 us  [body(): pl.pallas_call(functools.partial(kernel, parts, cores), out_shape=(out, o...]
where the time goes in v1:
time: 57.2 us; the launch traced here: 56.9 us
  Pallas kernels  52.7 us (92%)
  local copies, waits for them, and re-layouts  2.9 us (5%)
  between operations  1.31 us (2%)
    pallas_call x1, Pallas kernels, body(): pl.pallas_call(functools.partial(kernel, parts, cores), out_shape=(out, o...  52.7 us
    unnamed x6, local copies, waits for them, and re-layouts  2.29 us

profile of v1, /device:TPU:0, one launch (start us, length us, event | category | flops | bytes accessed | tf_op | source)
XLA Modules:
  0.0 56.9 jit_solution(633031988104566206)
XLA Ops:
  0.6 0.0 copy-start.1
  1.3 0.0 copy-done.1
  1.3 0.6 %reshape.51.list_ref = s32[6,2,128]{2,1,0:T(2,128)} reshape(s32[6,256]{1,0:T(8,128)S(1)} %copy-done.1) | data formatting | bytes 12288 | tf_op jit(solution)/shard_map/reshape | solution.py:589
  1.9 52.7 %shard_map.104 = (f32[256,128]{1,0:T(8,128)}, f32[256,128]{1,0:T(8,128)}) custom-call(s32[1]{0:T(128)S(6)} %copy.17.count_ref, f32[256,128]{1,0:T(8,128)} %bitcast.29, f32[256,128]{1,0:T(8,128)} %bitcast.30, f32[64,128]{1,0:T(8,128)} %bitcast.33, f32[96,3,128]{2,1,0:T(4,128)} %bitcast.26, s32[96,128]{1,0:T(8,128)} %bitcast.31, s32[96,128]{1,0:T(8,128)} %bitcast.32, ...), custom_call_target="tpu_custom_call" | custom-call | tf_op jit(solution)/shard_map/pallas_call | solution.py:539
  54.7 0.0 copy-start
  54.7 1.6 %copy.18 = f32[4,8192]{1,0:T(4,128)} copy(f32[4,8192]{1,0:T(4,128)} %bitcast.28) | data formatting | bytes 262144
  56.3 0.0 copy-done
  56.3 0.7 %copy.19 = f32[4,8192]{1,0:T(4,128)} copy(f32[4,8192]{1,0:T(4,128)S(1)} %bitcast.27) | data formatting | bytes 262144
Async XLA Ops:
  0.6 0.7 %copy-start.1 = (s32[6,256]{1,0:T(8,128)S(1)}, s32[6,256]{1,0:T(8,128)}, u32[]{:S(2)}) copy-start(s32[6,256]{1,0:T(8,128)} %param.16) | copy-start | bytes 18436
  54.7 1.6 %copy-start = (f32[256,128]{1,0:T(8,128)S(1)}, f32[256,128]{1,0:T(8,128)}, u32[]{:S(2)}) copy-start(f32[256,128]{1,0:T(8,128)} %get-tuple-element.5) | copy-start | bytes 393220

commit v2 on v1

v2 whole, which is shorter than its diff:
```python
import functools

import jax
import jax.numpy as jnp
from jax import lax
from jax.experimental import pallas as pl
from jax.experimental.pallas import tpu as pltpu
from jax.sharding import PartitionSpec as P

ITERS = 2
LANES = 128
MESH = pl.DeviceIdType.MESH
F32 = jnp.float32
BF16 = jnp.bfloat16


def take_lanes(source, index):
    return jnp.take_along_axis(source, index, axis=1, mode="promise_in_bounds")


def split(value):
    high = value.astype(BF16).astype(F32)
    rest = value - high
    middle = rest.astype(BF16).astype(F32)
    return high, middle, rest - middle


def woven(*queues):
    steps = [((i + 0.5) / len(q), n, f) for n, q in enumerate(queues) for i, f in enumerate(q)]
    for _, _, step in sorted(steps, key=lambda item: item[:2]):
        step()


def kernel(
    parts,
    cores,
    count_hbm,
    flow_hbm,
    source_hbm,
    volume_hbm,
    normal_hbm,
    owner_hbm,
    neighbour_hbm,
    list_hbm,
    halo_count_hbm,
    solution_ref,
    residual_ref,
    flow_ref,
    source_ref,
    volume_ref,
    normal_ref,
    owner_ref,
    neighbour_ref,
    list_ref,
    count_ref,
    halo_count_ref,
    list_at,
    list_col,
    found_rows,
    input_sem,
    own_lane,
    right_lane,
    right_kind,
    own_row,
    local_row,
    face_u,
    face_s,
    face_n,
    signed_hot,
    plain_hot,
    flux_rows,
    setup_rows,
    cell_rows,
    size_cells,
    fields,
    halo_rows,
    halo_mix,
    blocks,
    vecs,
    pair_out,
    pair_in,
    halo_out,
    halo_in,
    dot_out,
    dot_in,
    pair_send,
    pair_recv,
    halo_send,
    halo_recv,
    dot_send,
    dot_recv,
):
    me = lax.axis_index("cells")
    core = lax.axis_index("faces")
    other = (core + 1) % cores
    tiles = volume_ref.shape[0]
    pairs = tiles // 2
    groups = pairs // 8
    cells = tiles * LANES
    lists, width = list_ref.shape
    halves = width // LANES
    side = lists // 2
    lists_here = lists // cores
    period = halo_rows.shape[0] // (4 * halves)
    turns = pair_in.shape[0]

    def fetched(number, source, target):
        copy = pltpu.make_async_copy(source, target, input_sem.at[number])
        copy.start()
        return copy

    first_copies = [
        fetched(7, halo_count_hbm, halo_count_ref),
        fetched(6, list_hbm, list_ref),
        fetched(2, flow_hbm, flow_ref),
        fetched(4, source_hbm, source_ref),
        fetched(5, volume_hbm, volume_ref),
    ]
    index_copies = [
        fetched(8, count_hbm, count_ref),
        fetched(0, owner_hbm, owner_ref),
        fetched(1, neighbour_hbm, neighbour_ref),
    ]
    normals = [fetched(3, normal_hbm, normal_ref.at[pl.ds(0, 3 * pairs)])]

    barrier = pltpu.get_barrier_semaphore()

    def signal_entry(cell, face):
        pl.semaphore_signal(
            barrier,
            inc=1,
            device_id={"cells": cell, "faces": face},
            device_id_type=MESH,
        )

    for place in range(1, parts):
        offset = (place + 1) // 2 if place % 2 else parts - place // 2
        cell = lax.rem(me + offset, parts)
        for c in range(cores):
            signal_entry(cell, c)
    for step in range(1, cores):
        signal_entry(me, lax.rem(core + step, cores))

    row8 = lax.broadcasted_iota(jnp.int32, (8, LANES), 0)

    def look_up(which, half, wanted, hs, first):
        number = len(wanted)
        at = pl.ds(8 * (halves * which + half), 8)
        row, col = list_at[at, :], list_col[at, :]
        masks = [row == row8 + 8 * h for h in hs]
        for b, field in enumerate(wanted):
            place = pl.ds(8 * (halves * number * which + number * half + b), 8)
            found = jnp.zeros((8, LANES), F32) if first else found_rows[place, :]
            for h, mask in zip(hs, masks):
                found = jnp.where(mask, take_lanes(field(h), col), found)
            found_rows[place, :] = found

    def listed(which, place, number, limit, fills):
        rows = []
        for half in range(halves):
            used = lax.broadcasted_iota(jnp.int32, (1, LANES), 1) + half * LANES < limit
            for b, fill in enumerate(fills):
                at = pl.ds(8 * (halves * number * place + number * half + b), 8)
                found = jnp.sum(found_rows[at, :], axis=0, keepdims=True)
                rows.append(jnp.where(used, found, fill))
        return rows

    def send_halo(turn, rows, place):
        pitch = 8 if turn == 0 else 16
        for k in range(lists):
            offset = k + 1 if k < side else side - 1 - k
            for c in range(cores):
                pltpu.make_async_remote_copy(
                    src_ref=halo_out.at[turn, k, pl.ds(0, rows)],
                    dst_ref=halo_in.at[turn, place, pl.ds(k * pitch, rows)],
                    send_sem=halo_send.at[turn],
                    recv_sem=halo_recv.at[turn],
                    device_id={"cells": lax.rem(me + offset + parts, parts), "faces": c},
                    device_id_type=MESH,
                ).start()

    def halo_part(turn):
        if turn == 0:
            return halo_in.at[turn, 0, pl.ds(0, 8 * lists)]
        return halo_in.at[turn] if turn == 1 else halo_in.at[turn, 0]

    def wait_halo(turn):
        part = halo_part(turn)
        pltpu.make_async_copy(part, part, halo_recv.at[turn]).wait()

    def halo_row(turn, place, row):
        pitch = 8 if turn == 0 else 16
        return halo_in[turn, place, pl.ds(row, lists, stride=pitch), :]

    def halo_sums(turn, number):
        return [
            [
                halo_row(turn, 0, half * number + b) + halo_row(turn, 1, half * number + b)
                for half in range(halves)
            ]
            for b in range(number)
        ]

    def look_up_all(turn, number, hs, first):
        def step(k, half):
            wanted = [functools.partial(partial_field, turn, b) for b in range(number)]
            return lambda: look_up(k, half, wanted, hs, first)

        return [step(k, half) for k in range(lists) for half in range(halves)]

    def put_listed(turn, fills):
        number = len(fills)
        rows = 8 if number * halves <= 8 else 16
        for k in range(lists):
            found = listed(k, k, number, halo_count_ref[k], fills)
            spare = rows - len(found)
            if spare:
                found.append(jnp.zeros((spare, LANES), F32))
            halo_out[turn, k, :rows] = jnp.concatenate(found, axis=0)
        return rows

    def pair_copy(turn, rows):
        part = pl.ds(0, rows)
        copy = pltpu.make_async_remote_copy(
            src_ref=pair_out.at[turn, part],
            dst_ref=pair_in.at[turn, part],
            send_sem=pair_send.at[turn],
            recv_sem=pair_recv.at[turn],
            device_id={"cells": me, "faces": other},
            device_id_type=MESH,
        )
        copy.start()
        return copy

    def start_dots(turn, partials):
        at = lax.broadcasted_iota(jnp.int32, (1, LANES), 1)
        packed = jnp.zeros((1, LANES), F32)
        for d, p in enumerate(partials):
            row = jnp.sum(p.reshape(tiles // 8, 8, LANES).sum(axis=0), axis=0, keepdims=True)
            packed = jnp.where(at == d, jnp.sum(row, axis=1, keepdims=True), packed)
        dot_out[turn] = packed

        @pl.when(core == 0)
        def _():
            dot_in[turn, me] = packed
            for place in range(1, parts):
                offset = (place + 1) // 2 if place % 2 else parts - place // 2
                for c in range(cores):
                    send_dots(turn, lax.rem(me + offset, parts), c)
            for c in range(1, cores):
                send_dots(turn, me, c)

    def send_dots(turn, cell, face):
        pltpu.make_async_remote_copy(
            src_ref=dot_out.at[turn],
            dst_ref=dot_in.at[turn, me],
            send_sem=dot_send.at[turn],
            recv_sem=dot_recv.at[turn],
            device_id={"cells": cell, "faces": face},
            device_id_type=MESH,
        ).start()

    def wait_dots(turn, number):
        @pl.when(core == 0)
        def _():
            part = dot_in.at[turn, pl.ds(0, parts - 1)]
            pltpu.make_async_copy(part, part, dot_recv.at[turn]).wait()

        @pl.when(core != 0)
        def _():
            part = dot_in.at[turn, pl.ds(0, parts)]
            pltpu.make_async_copy(part, part, dot_recv.at[turn]).wait()

        total = dot_in[turn, 0]
        for q in range(1, parts):
            total = total + dot_in[turn, q]
        return [jnp.broadcast_to(total[:, d : d + 1], (1, LANES)) for d in range(number)]

    def put_field(values):
        for b, value in enumerate(values):
            fields[b, pl.ds(0, tiles), :] = value
            fields[b, pl.ds(tiles, 1), :] = value[0:1]

    def put_halo(values):
        for b, value in enumerate(values):
            for half in range(halves):
                halo_mix[pl.ds(halves * b + half, lists, stride=8), :] = value[half]
        for t in range(period):
            mixed = halo_mix[pl.ds(8 * (t % lists), 8), :]
            halo_rows[pl.ds(t, 8, stride=period), :] = mixed

    def sides(g, j, b):
        here = pl.ds(g * 8, 8)
        left_at = own_lane[j, here, :]
        right_at = right_lane[j, here, :]
        kind = right_kind[j, here, :]

        def of_tile(odd):
            first = 16 * g + odd
            halo_first = (16 * g) % lists + odd
            low = fields[b, pl.ds(first, 8, stride=2), :]
            high = fields[b, pl.ds(first + 1, 8, stride=2), :]
            halo_low = halo_rows[pl.ds(2 * b * period + halo_first, 8, stride=2), :]
            halo_high = halo_rows[pl.ds((2 * b + 1) * period + halo_first, 8, stride=2), :]
            left = take_lanes(low, left_at)
            right = jnp.where(
                kind < 2,
                jnp.where(kind == 0, take_lanes(low, right_at), take_lanes(high, right_at)),
                jnp.where(
                    kind == 2, take_lanes(halo_low, right_at), take_lanes(halo_high, right_at)
                ),
            )
            return left, right

        if j == 0:
            return of_tile(0)
        if j == 2:
            return of_tile(1)
        early = lax.broadcasted_iota(jnp.int32, (8, LANES), 1) < LANES // 2
        left_a, right_a = of_tile(0)
        left_b, right_b = of_tile(1)
        return jnp.where(early, left_a, left_b), jnp.where(early, right_a, right_b)

    def put_flux(ref, g, j, b, value):
        for part, piece in enumerate(split(value)):
            row = 4 * part + b if b < 4 else 12 + part
            ref[j, pl.ds(128 * g + row, 8, stride=16), :] = piece

    def tile_rows(rows_ref, u, odd):
        at = pl.ds(u * 16, 16)
        middle = rows_ref[1, at, :]
        if odd:
            middle = pltpu.roll(middle, LANES // 2, 1)
        rows = jnp.concatenate([rows_ref[2 * odd, at, :], middle], axis=1)
        return rows[:, : 3 * LANES // 2].astype(BF16)

    def added(rows, hot):
        return lax.dot_general(
            rows, hot, (((1,), (0,)), ((), ())), preferred_element_type=F32
        )

    def scatter(u, odd):
        result = added(tile_rows(flux_rows, u, odd), signed_hot[2 * u + odd])
        result = result[:8] + result[8:]
        at = u * 16 + odd * 8
        cell_rows[0, pl.ds(at, 8), :] = result[:, :LANES]
        cell_rows[1, pl.ds(at + 8, 8), :] = result[:, LANES:]

    def scatter_size(u, odd):
        rows = tile_rows(setup_rows, u, odd)
        at = u * 16 + odd * 8
        result = added(rows, signed_hot[2 * u + odd])
        low = lax.broadcasted_iota(jnp.int32, (8, 2 * LANES), 0) < 4
        summed = result[:8] + jnp.where(low, result[8:], 0.0)
        cell_rows[0, pl.ds(at, 8), :] = summed[:, :LANES]
        cell_rows[1, pl.ds(at + 8, 8), :] = summed[:, LANES:]
        size_cells[0, pl.ds(at, 8), :] = added(rows, plain_hot[2 * u + odd])[8:]
        size_cells[1, pl.ds(at + 8, 8), :] = -result[8:, LANES:]

    def collect(turn, g, number):
        def rows(cells_ref, place, first):
            return cells_ref[place, pl.ds(first, 16, stride=8), :]

        for b in range(min(number, 4)):
            first = 128 * g + b
            low = rows(cell_rows, 0, first) + rows(cell_rows, 0, first + 4)
            high = rows(cell_rows, 1, first) + rows(cell_rows, 1, first + 4)
            pair_out[turn, pl.ds(tiles * b + 16 * g, 16), :] = low + high
        if number > 4:
            pieces = [
                rows(size_cells, 0, 128 * g + row) + rows(size_cells, 1, 128 * g + row)
                for row in (4, 5, 6)
            ]
            total = pieces[0] + pieces[1] + pieces[2]
            pair_out[turn, pl.ds(4 * tiles + 16 * g, 16), :] = total
        if g == groups - 1:
            end = pl.ds(8 * tiles, 8)
            pair_out[turn, pl.ds(number * tiles, 8), :] = cell_rows[1, end, :]
            if number > 4:
                pair_out[turn, pl.ds(number * tiles + 8, 8), :] = size_cells[1, end, :]

    def wrapped(ref, turn, b):
        number = 5 if turn == 0 else 4

        def row(at):
            return ref[turn, pl.ds(number * tiles + at, 1), :]

        if b < 4:
            return row(b) + row(b + 4)
        return row(12) + row(13) + row(14)

    def partial_field(turn, b, h):
        found = pair_out[turn, pl.ds(tiles * b + 8 * h, 8), :]
        if h == 0:
            found = found + jnp.where(row8 == 0, wrapped(pair_out, turn, b), 0.0)
        return found

    def pair_sums(turn, copy, number):
        copy.wait_recv()
        first = lax.broadcasted_iota(jnp.int32, (tiles, LANES), 0) == 0
        sums = []
        for b in range(number):
            rows = pl.ds(tiles * b, tiles)
            wrap = wrapped(pair_out, turn, b) + wrapped(pair_in, turn, b)
            total = pair_out[turn, rows, :] + pair_in[turn, rows, :]
            sums.append(total + jnp.where(first, wrap, 0.0))
        return sums

    sent = []

    def flux_steps(g):
        def step(j):
            here = pl.ds(g * 8, 8)
            u = face_u[j, here, :]
            s = face_s[j, here, :]
            n = [face_n[i, j, here, :] for i in range(3)]
            both = [sides(g, j, b) for b in range(4)]
            total = [left + right for left, right in both]
            jump = [s * (right - left) for left, right in both]
            for i in range(3):
                put_flux(flux_rows, g, j, i, u * total[i] + n[i] * total[3] - jump[i])
            last = n[0] * total[0] + n[1] * total[1] + n[2] * total[2] - jump[3]
            put_flux(flux_rows, g, j, 3, last)

        return [functools.partial(step, j) for j in range(3)]

    def over_groups(turn, faces, spread, number, search):
        for stage in range(groups + 2):
            queues = []
            if stage < groups:
                queues.append(faces(stage))
            if 1 <= stage <= groups:
                queues.append(
                    [
                        functools.partial(spread, 8 * (stage - 1) + i, odd)
                        for i in range(8)
                        for odd in range(2)
                    ]
                )
            if search and stage >= 2:
                hs = [2 * (stage - 2), 2 * (stage - 2) + 1]
                if stage == 2:
                    hs = hs[1:]
                if stage == groups + 1:
                    hs = hs + [0]
                queues.append(look_up_all(turn, number, hs, stage == 2))
            woven(*queues)
            if 1 <= stage <= groups:
                collect(turn, stage - 1, number)
        if search:
            rows = put_listed(turn + 1, [0.0] * number)
            send_halo(turn + 1, rows, core)
        copy = pair_copy(turn, number * tiles + 8 * (number - 3))
        sent.append(copy)
        return copy

    def apply_matrix(turn, values):
        copy = over_groups(turn, flux_steps, scatter, 4, True)
        sums = pair_sums(turn, copy, 4)
        volume = volume_ref[...]
        return [volume * values[b] + sums[b] for b in range(4)]

    def halo_image(turn, halos):
        wait_halo(turn)
        sums = halo_sums(turn, 4)
        return [
            [halo_volume[half] * halos[b][half] + sums[b][half] for half in range(halves)]
            for b in range(4)
        ]

    def solved(w, rvd, rschur, n):
        pressure = (w[3] - (n[0] * w[0] + n[1] * w[1] + n[2] * w[2]) * rvd) * rschur
        return [(w[i] - n[i] * pressure) * rvd for i in range(3)] + [pressure]

    def precondition(w):
        return solved(w, blocks[0], blocks[1], [blocks[2 + i] for i in range(3)])

    def precondition_halo(w):
        by_half = [
            solved([w[b][half] for b in range(4)], *halo_blocks[half]) for half in range(halves)
        ]
        return [[by_half[half][b] for half in range(halves)] for b in range(4)]

    def inverse(volume, sums):
        rvd = 1.0 / (volume + sums[0] + sums[4])
        n = sums[1:4]
        norm = n[0] * n[0] + n[1] * n[1] + n[2] * n[2]
        return rvd, 1.0 / (volume + sums[4] - norm * rvd), n

    def load(which):
        return [vecs[which, b] for b in range(4)]

    def save(which, values):
        for b in range(4):
            vecs[which, b] = values[b]

    def dot(a, b):
        return a[0] * b[0] + a[1] * b[1] + a[2] * b[2] + a[3] * b[3]

    def combine(a, scale, b):
        return [x + scale * y for x, y in zip(a, b)]

    def combine_halo(a, scale, b):
        return [[x + scale * y for x, y in zip(p, q)] for p, q in zip(a, b)]

    def load_source():
        return [source_ref[pl.ds(b, tiles, stride=4), :] for b in range(4)]

    def first_field(b, h):
        if b == 7:
            return volume_ref[pl.ds(8 * h, 8), :]
        ref, component = (flow_ref, b) if b < 3 else (source_ref, b - 3)
        return ref[pl.ds(32 * h + component, 8, stride=4), :]

    for copy in first_copies:
        copy.wait()
    for k in range(lists):
        for half in range(halves):
            cell = list_ref[k : k + 1, half * LANES : (half + 1) * LANES]
            cell = jnp.broadcast_to(cell, (8, LANES))
            at = pl.ds(8 * (halves * k + half), 8)
            list_at[at, :] = cell // LANES
            list_col[at, :] = cell - cell // LANES * LANES
    every = list(range(tiles // 8))

    @pl.when(core == 0)
    def _():
        wanted = [functools.partial(first_field, b) for b in range(3)]
        for k in range(lists):
            for half in range(halves):
                look_up(k, half, wanted, every, True)
        put_listed(0, [0.0] * 3)

    @pl.when(core == cores - 1)
    def _():
        wanted = [functools.partial(first_field, b) for b in range(3, 8)]
        for k in range(lists):
            for half in range(halves):
                look_up(k, half, wanted, every, True)
        put_listed(turns, [0.0] * 4 + [1.0])

    pl.semaphore_wait(barrier, parts * cores - 1)

    @pl.when(core == 0)
    def _():
        send_halo(0, 8, 0)

    @pl.when(core == cores - 1)
    def _():
        send_halo(turns, 16, 0)

    lane = lax.broadcasted_iota(jnp.int32, (pairs, LANES), 1)
    pair_id = lax.broadcasted_iota(jnp.int32, (pairs, LANES), 0)
    late = lane >= LANES // 2
    for copy in index_copies:
        copy.wait()
    count = count_ref[0]
    for j in range(3):
        tile = 2 * pair_id + (0 if j == 0 else 1)
        if j == 1:
            tile = 2 * pair_id + late.astype(jnp.int32)
        owner = owner_ref[pl.ds(j, pairs, stride=3), :]
        beside = neighbour_ref[pl.ds(j, pairs, stride=3), :]
        live = (3 * pair_id + j) * LANES + lane < count
        is_local = beside < cells
        column = beside - tile * LANES
        column = jnp.where(column < 0, column + cells, column)
        slot = beside - cells - (tile % lists) * width
        place = jnp.where(is_local, column, slot)
        upper = place >= LANES
        own = owner - tile * LANES
        own_lane[j] = own
        right_lane[j] = jnp.where(upper, place - LANES, place)
        right_kind[j] = jnp.where(is_local, 0, 2) + upper.astype(jnp.int32)
        own_row[j] = jnp.where(live, own, -1).astype(F32)
        local_row[j] = jnp.where(live & is_local, column, -1).astype(F32)

    cell_id = lax.broadcasted_iota(jnp.int32, (LANES, LANES), 1).astype(F32).astype(BF16)
    one, zero = jnp.ones((), BF16), jnp.zeros((), BF16)

    def by_face(rows):
        flat = rows[...].reshape(3 * pairs, LANES)
        spare = -(3 * pairs) % LANES
        flat = jnp.concatenate([flat, jnp.zeros((spare, LANES), F32)], axis=0)
        return flat.T.astype(BF16)

    own_faces, local_faces = by_face(own_row), by_face(local_row)

    def hot_of(column):
        return jnp.where(cell_id == column, one, zero)

    for u in range(pairs):
        for j in range(3):
            at = j * pairs + u
            own = jnp.broadcast_to(own_faces[:, at : at + 1], (LANES, LANES))
            local = jnp.broadcast_to(local_faces[:, at : at + 1], (LANES, LANES))
            own_hot, local_hot = hot_of(own), hot_of(local)
            low = own_hot - local_hot
            high = -hot_of(local - LANES)
            plain = own_hot + local_hot
            half = LANES // 2
            if j == 1:
                places = [(2 * u, LANES, 0, half), (2 * u + 1, LANES, half, LANES)]
            else:
                places = [(2 * u + j // 2, 0, 0, LANES)]
            for tile, row, first, last in places:
                rows = slice(row, row + last - first)
                signed_hot[tile, rows, :LANES] = low[first:last]
                signed_hot[tile, rows, LANES:] = high[first:last]
                plain_hot[tile, rows, :] = plain[first:last]

    setup_rows[...] = jnp.zeros_like(setup_rows)
    flux_rows[...] = jnp.zeros_like(flux_rows)
    cell_rows[1, :8, :] = jnp.zeros((8, LANES), F32)
    size_cells[1, :8, :] = jnp.zeros((8, LANES), F32)
    for copy in normals:
        copy.wait()

    put_field([flow_ref[pl.ds(b, tiles, stride=4), :] for b in range(3)])
    wait_halo(0)
    put_halo([[halo_row(0, 0, half * 3 + b) for half in range(halves)] for b in range(3)])

    def face_steps(g):
        def step(j):
            here = pl.ds(g * 8, 8)
            n = [normal_ref[pl.ds(24 * g + j, 8, stride=3), i, :] for i in range(3)]
            both = [sides(g, j, b) for b in range(3)]
            total = [left + right for left, right in both]
            u = 0.5 * (n[0] * total[0] + n[1] * total[1] + n[2] * total[2])
            s = jnp.abs(u) + 2.0 * jnp.sqrt(n[0] * n[0] + n[1] * n[1] + n[2] * n[2])
            u, s = 0.5 * u, 0.5 * s
            n = [0.5 * n[i] for i in range(3)]
            face_u[j, here, :] = u
            face_s[j, here, :] = s
            put_flux(setup_rows, g, j, 0, u)
            for i in range(3):
                face_n[i, j, here, :] = n[i]
                put_flux(setup_rows, g, j, 1 + i, n[i])
            put_flux(setup_rows, g, j, 4, s)

        return [functools.partial(step, j) for j in range(3)]

    copy = over_groups(0, face_steps, scatter_size, 5, True)
    rvd, rschur, coupling = inverse(volume_ref[...], pair_sums(0, copy, 5))
    blocks[0] = rvd
    blocks[1] = rschur
    for i in range(3):
        blocks[2 + i] = coupling[i]

    shadow = load_source()
    pre = precondition(shadow)
    put_field(pre)
    wait_halo(turns)

    def first_halo(b):
        return [halo_row(turns, 0, half * 5 + b) for half in range(halves)]

    halo_volume = first_halo(4)
    halo_residual = [first_halo(b) for b in range(4)]
    wait_halo(1)
    sums = halo_sums(1, 5)
    halo_blocks = [
        inverse(halo_volume[half], [sums[b][half] for b in range(5)]) for half in range(halves)
    ]
    halo_pre = precondition_halo(halo_residual)
    put_halo(halo_pre)

    V, T, W, MIDDLE, SECOND, SUM = range(6)
    image = apply_matrix(1, pre)
    shadow = load_source()
    start_dots(0, [dot(shadow, shadow), dot(shadow, image)])
    save(V, image)
    pre = precondition(image)
    put_field(pre)
    halo_v = halo_image(2, halo_pre)
    halo_pre = precondition_halo(halo_v)
    put_halo(halo_pre)

    twice = apply_matrix(2, pre)
    rho, shadow_image = wait_dots(0, 2)
    alpha = rho / shadow_image
    shadow, image = load_source(), load(V)
    middle = combine(shadow, -alpha, image)
    second = combine(image, -alpha, twice)
    start_dots(
        1, [dot(second, middle), dot(second, second), dot(shadow, middle), dot(shadow, second)]
    )
    save(T, twice)
    save(MIDDLE, middle)
    save(SECOND, second)
    pre = precondition(twice)
    put_field(pre)
    halo_t = halo_image(3, halo_pre)
    halo_pre = precondition_halo(halo_t)
    put_halo(halo_pre)

    thrice = apply_matrix(3, pre)
    second_mid, second_sq, shadow_mid, shadow_second = wait_dots(1, 4)
    omega = second_mid / second_sq
    rho_next = shadow_mid - omega * shadow_second
    beta = rho_next / rho * (alpha / omega)
    shadow, image, twice, middle, second = (
        load_source(),
        load(V),
        load(T),
        load(MIDDLE),
        load(SECOND),
    )
    residual = combine(middle, -omega, second)
    image_residual = combine(second, -omega, combine(twice, -alpha, thrice))
    direction = combine(residual, beta, combine(shadow, -omega, image))
    next_image = combine(image_residual, beta, combine(image, -omega, twice))
    start_dots(2, [dot(shadow, next_image)])
    save(V, next_image)
    save(T, residual)
    save(W, image_residual)
    save(SUM, combine([alpha * x for x in shadow], omega, middle))
    save(MIDDLE, direction)
    pre = precondition(next_image)
    put_field(pre)
    halo_w = halo_image(4, halo_pre)
    halo_second = combine_halo(halo_v, -alpha, halo_t)
    halo_next = combine_halo(
        combine_halo(halo_second, -omega, combine_halo(halo_t, -alpha, halo_w)),
        beta,
        combine_halo(halo_v, -omega, halo_t),
    )
    put_halo(precondition_halo(halo_next))

    copy = over_groups(4, flux_steps, scatter, 4, False)
    (shadow_image,) = wait_dots(2, 1)
    alpha = rho_next / shadow_image
    middle = combine(load(T), -alpha, load(V))
    save(MIDDLE, combine(load(SUM), alpha, load(MIDDLE)))
    volume = volume_ref[...]
    base = combine(load(W), -alpha, [volume * v for v in pre])
    second = combine(base, -alpha, pair_sums(4, copy, 4))
    start_dots(3, [dot(second, middle), dot(second, second)])
    known = precondition(load(MIDDLE))
    pre_mid = precondition(middle)
    second_mid, second_sq = wait_dots(3, 2)
    omega = second_mid / second_sq
    for b in range(4):
        solution_ref[pl.ds(b, tiles, stride=4), :] = known[b] + omega * pre_mid[b]
        residual_ref[pl.ds(b, tiles, stride=4), :] = middle[b] - omega * second[b]

    @pl.when(core == 0)
    def _():
        part = halo_in.at[0, 0]
        pltpu.make_async_copy(part, part, halo_send.at[0]).wait()
        for turn in range(dot_in.shape[0]):
            for part in (dot_in.at[turn, pl.ds(0, parts - 1)], dot_in.at[turn, pl.ds(0, parts)]):
                pltpu.make_async_copy(part, part, dot_send.at[turn]).wait()

    @pl.when(core == cores - 1)
    def _():
        part = halo_in.at[turns]
        pltpu.make_async_copy(part, part, halo_send.at[turns]).wait()

    for turn in range(1, turns):
        part = halo_part(turn)
        pltpu.make_async_copy(part, part, halo_send.at[turn]).wait()
    for copy in sent:
        copy.wait_send()


def body(
    flow_state,
    source_term,
    volume_rate,
    face_normal,
    face_owner,
    face_neighbour,
    face_count,
    send_list,
    halo_count,
):
    parts = lax.axis_size("cells")
    cores = lax.axis_size("faces")
    cells = flow_state.shape[1]
    tiles = cells // LANES
    pairs = tiles // 2
    groups = pairs // 8
    face_rows = face_owner.shape[0] // LANES
    lists, width = send_list.shape
    period = -(-(lists + 16) // 8) * 8
    turns = 1 + 2 * ITERS

    def by_tile(field):
        return field.reshape(4, tiles, LANES).transpose(1, 0, 2).reshape(4 * tiles, LANES)

    def by_component(field):
        return field.reshape(tiles, 4, LANES).transpose(1, 0, 2).reshape(4, cells)

    vmem = pl.BlockSpec(memory_space=pltpu.VMEM)
    hbm = pl.BlockSpec(memory_space=pltpu.HBM)
    ints = pltpu.VMEM((3, pairs, LANES), jnp.int32)
    floats = pltpu.VMEM((3, pairs, LANES), F32)
    hot = pltpu.VMEM((tiles, 3 * LANES // 2, 2 * LANES), BF16)
    out = jax.ShapeDtypeStruct((4 * tiles, LANES), F32)
    solved, left = pl.pallas_call(
        functools.partial(kernel, parts, cores),
        out_shape=(out, out),
        in_specs=[hbm] * 9,
        out_specs=(vmem, vmem),
        scratch_shapes=[
            pltpu.VMEM((4 * tiles, LANES), F32),
            pltpu.VMEM((4 * tiles, LANES), F32),
            pltpu.VMEM((tiles, LANES), F32),
            pltpu.VMEM((face_rows + 8, 3, LANES), F32),
            pltpu.VMEM((face_rows, LANES), jnp.int32),
            pltpu.VMEM((face_rows, LANES), jnp.int32),
            pltpu.VMEM((lists, width), jnp.int32),
            pltpu.SMEM((1,), jnp.int32),
            pltpu.SMEM((lists,), jnp.int32),
            pltpu.VMEM((8 * lists * width // LANES, LANES), jnp.int32),
            pltpu.VMEM((8 * lists * width // LANES, LANES), jnp.int32),
            pltpu.VMEM((40 * lists * width // LANES, LANES), F32),
            pltpu.SemaphoreType.DMA((9,)),
            ints,
            ints,
            ints,
            floats,
            floats,
            floats,
            floats,
            pltpu.VMEM((3, 3, pairs, LANES), F32),
            hot,
            pltpu.VMEM((tiles, 3 * LANES // 2, LANES), BF16),
            pltpu.VMEM((3, 16 * pairs, LANES), F32),
            pltpu.VMEM((3, 16 * pairs, LANES), F32),
            pltpu.VMEM((2, 8 * tiles + 8, LANES), F32),
            pltpu.VMEM((2, 8 * tiles + 8, LANES), F32),
            pltpu.VMEM((4, tiles + 8, LANES), F32),
            pltpu.VMEM((8 * period, LANES), F32),
            pltpu.VMEM((8 * lists, LANES), F32),
            pltpu.VMEM((5, tiles, LANES), F32),
            pltpu.VMEM((6, 4, tiles, LANES), F32),
            pltpu.VMEM((turns, 5 * tiles + 16, LANES), F32),
            pltpu.VMEM((turns, 5 * tiles + 16, LANES), F32),
            pltpu.VMEM((turns + 1, lists, 16, LANES), F32),
            pltpu.VMEM((turns + 1, cores, 16 * lists, LANES), F32),
            pltpu.VMEM((turns + 8, 1, LANES), F32),
            pltpu.VMEM((turns - 1, parts + 8, 1, LANES), F32),
            pltpu.SemaphoreType.DMA((turns,)),
            pltpu.SemaphoreType.DMA((turns,)),
            pltpu.SemaphoreType.DMA((turns + 1,)),
            pltpu.SemaphoreType.DMA((turns + 1,)),
            pltpu.SemaphoreType.DMA((turns - 1,)),
            pltpu.SemaphoreType.DMA((turns - 1,)),
        ],
        compiler_params=pltpu.CompilerParams(
            collective_id=0, has_side_effects=True, vmem_limit_bytes=56 * 1024 * 1024
        ),
    )(
        face_count,
        by_tile(flow_state),
        by_tile(source_term),
        volume_rate.reshape(tiles, LANES),
        face_normal.reshape(3, face_rows, LANES).transpose(1, 0, 2),
        face_owner.reshape(face_rows, LANES),
        face_neighbour.reshape(face_rows, LANES),
        send_list,
        halo_count,
    )
    return by_component(solved), by_component(left)


def solution(mesh):
    in_specs = (
        P(None, "cells"),
        P(None, "cells"),
        P("cells"),
        P(None, ("cells", "faces")),
        P(("cells", "faces")),
        P(("cells", "faces")),
        P(("cells", "faces")),
        P("cells", None),
        P("cells"),
    )
    out_specs = (P(None, "cells"), P(None, "cells"))
    return jax.shard_map(body, mesh=mesh, in_specs=in_specs, out_specs=out_specs, check_vma=False)
```

time: 57.2 us -> 48.1 us (0.84)
  Pallas kernels: 52.7 us -> 44.4 us
  local copies, waits for them, and re-layouts: 2.9 us -> 2.26 us
    pallas_call x1, Pallas kernels: 52.7 us -> 44.4 us  [body(): pl.pallas_call(functools.partial(kernel, parts, cores), out_shape=(out, o...]
    reshape x1 -> x0, local copies, waits for them, and re-layouts: 0.6 us -> none  [body(): send_list.reshape(lists, width // LANES, LANES)]
    unnamed x6 -> x4, local copies, waits for them, and re-layouts: 2.29 us -> 2.26 us
where the time goes in v2:
time: 48.1 us; the launch traced here: 47.9 us
  Pallas kernels  44.4 us (92%)
  local copies, waits for them, and re-layouts  2.26 us (5%)
  between operations  1.3 us (3%)
    pallas_call x1, Pallas kernels, body(): pl.pallas_call(functools.partial(kernel, parts, cores), out_shape=(out, o...  44.4 us
    unnamed x4, local copies, waits for them, and re-layouts  2.26 us

profile of v2, /device:TPU:0, one launch (start us, length us, event | category | flops | bytes accessed | tf_op | source)
XLA Modules:
  0.0 47.9 jit_solution(14645271507772731601)
XLA Ops:
  1.3 44.4 %shard_map.104 = (f32[256,128]{1,0:T(8,128)}, f32[256,128]{1,0:T(8,128)}) custom-call(s32[1]{0:T(128)S(6)} %copy.17.count_hbm, f32[256,128]{1,0:T(8,128)} %bitcast.29, f32[256,128]{1,0:T(8,128)} %bitcast.30, f32[64,128]{1,0:T(8,128)} %bitcast.33, f32[96,3,128]{2,1,0:T(4,128)} %bitcast.26, s32[96,128]{1,0:T(8,128)} %bitcast.31, s32[96,128]{1,0:T(8,128)} %bitcast.32, ...), custom_call_target="tpu_custom_call" | custom-call | tf_op jit(solution)/shard_map/pallas_call | solution.py:801
  45.6 0.0 copy-start
  45.6 1.6 %copy.18 = f32[4,8192]{1,0:T(4,128)} copy(f32[4,8192]{1,0:T(4,128)} %bitcast.28) | data formatting | bytes 262144
  47.3 0.0 copy-done
  47.3 0.7 %copy.19 = f32[4,8192]{1,0:T(4,128)} copy(f32[4,8192]{1,0:T(4,128)S(1)} %bitcast.27) | data formatting | bytes 262144
Async XLA Ops:
  45.6 1.6 %copy-start = (f32[256,128]{1,0:T(8,128)S(1)}, f32[256,128]{1,0:T(8,128)}, u32[]{:S(2)}) copy-start(f32[256,128]{1,0:T(8,128)} %get-tuple-element.5) | copy-start | bytes 393220

commit v3 on v2

--- a/solution.py
+++ b/solution.py
@@ -67,11 +67,13 @@
     face_s,
     face_n,
     signed_hot,
-    plain_hot,
+    own_hot,
     flux_rows,
     setup_rows,
     cell_rows,
     size_cells,
+    own_cells,
+    local_sums,
     fields,
     halo_rows,
     halo_mix,
@@ -103,6 +105,9 @@
     lists_here = lists // cores
     period = halo_rows.shape[0] // (4 * halves)
     turns = pair_in.shape[0]
+    offsets = [k + 1 if k < side else side - 1 - k for k in range(lists)]
+    sooner = [k for k in range(lists) if offsets[k] % 2]
+    later = [k for k in range(lists) if offsets[k] % 2 == 0]
 
     def fetched(number, source, target):
         copy = pltpu.make_async_copy(source, target, input_sem.at[number])
@@ -155,27 +160,44 @@
                 found = jnp.where(mask, take_lanes(field(h), col), found)
             found_rows[place, :] = found
 
-    def listed(which, place, number, limit, fills):
-        rows = []
-        for half in range(halves):
-            used = lax.broadcasted_iota(jnp.int32, (1, LANES), 1) + half * LANES < limit
-            for b, fill in enumerate(fills):
-                at = pl.ds(8 * (halves * number * place + number * half + b), 8)
-                found = jnp.sum(found_rows[at, :], axis=0, keepdims=True)
-                rows.append(jnp.where(used, found, fill))
-        return rows
-
-    def send_halo(turn, rows, place):
+    def row_sums(blocks_of):
+        shift, level = 1, blocks_of
+        while len(level) > 1:
+            mask = (row8 // shift) % 2 == 0
+            level = [
+                jnp.where(mask, x, y) + pltpu.roll(jnp.where(mask, y, x), 8 - shift, 0)
+                for x, y in zip(level[::2], level[1::2])
+            ]
+            shift *= 2
+        return level[0]
+
+    def listed(k, fills):
+        number = len(fills)
+        flat = [found_rows[pl.ds(8 * (halves * number * k + i), 8), :] for i in range(halves * number)]
+        flat += [jnp.zeros((8, LANES), F32)] * (-len(flat) % 8)
+        slot = lax.broadcasted_iota(jnp.int32, (8, LANES), 1)
+        limit = halo_count_ref[k]
+        tiles_of = []
+        for first in range(0, len(flat), 8):
+            row = row8 + first
+            half = row // number
+            used = slot + half * LANES < limit
+            fill = jnp.zeros((8, LANES), F32)
+            if fills[-1]:
+                fill = jnp.where(row % number == number - 1, fills[-1], 0.0)
+            tiles_of.append(jnp.where(used, row_sums(flat[first : first + 8]), fill))
+        return tiles_of
+
+    def send_halo(turn, rows, place, which):
         pitch = 8 if turn == 0 else 16
-        for k in range(lists):
-            offset = k + 1 if k < side else side - 1 - k
+        for k in which:
             for c in range(cores):
                 pltpu.make_async_remote_copy(
                     src_ref=halo_out.at[turn, k, pl.ds(0, rows)],
                     dst_ref=halo_in.at[turn, place, pl.ds(k * pitch, rows)],
                     send_sem=halo_send.at[turn],
                     recv_sem=halo_recv.at[turn],
-                    device_id={"cells": lax.rem(me + offset + parts, parts), "faces": c},
+                    device_id={"cells": lax.rem(me + offsets[k] + parts, parts), "faces": c},
                     device_id_type=MESH,
                 ).start()
 
@@ -201,23 +223,18 @@
             for b in range(number)
         ]
 
-    def look_up_all(turn, number, hs, first):
+    def look_up_all(turn, number, hs, first, which):
         def step(k, half):
             wanted = [functools.partial(partial_field, turn, b) for b in range(number)]
             return lambda: look_up(k, half, wanted, hs, first)
 
-        return [step(k, half) for k in range(lists) for half in range(halves)]
-
-    def put_listed(turn, fills):
-        number = len(fills)
-        rows = 8 if number * halves <= 8 else 16
-        for k in range(lists):
-            found = listed(k, k, number, halo_count_ref[k], fills)
-            spare = rows - len(found)
-            if spare:
-                found.append(jnp.zeros((spare, LANES), F32))
-            halo_out[turn, k, :rows] = jnp.concatenate(found, axis=0)
-        return rows
+        return [step(k, half) for k in which for half in range(halves)]
+
+    def put_listed(turn, fills, which):
+        for k in which:
+            for i, rows in enumerate(listed(k, fills)):
+                halo_out[turn, k, pl.ds(8 * i, 8)] = rows
+        return 8 * (-(-halves * len(fills) // 8))
 
     def pair_copy(turn, rows):
         part = pl.ds(0, rows)
@@ -289,37 +306,50 @@
             mixed = halo_mix[pl.ds(8 * (t % lists), 8), :]
             halo_rows[pl.ds(t, 8, stride=period), :] = mixed
 
-    def sides(g, j, b):
-        here = pl.ds(g * 8, 8)
-        left_at = own_lane[j, here, :]
-        right_at = right_lane[j, here, :]
-        kind = right_kind[j, here, :]
-
-        def of_tile(odd):
-            first = 16 * g + odd
-            halo_first = (16 * g) % lists + odd
-            low = fields[b, pl.ds(first, 8, stride=2), :]
-            high = fields[b, pl.ds(first + 1, 8, stride=2), :]
-            halo_low = halo_rows[pl.ds(2 * b * period + halo_first, 8, stride=2), :]
-            halo_high = halo_rows[pl.ds((2 * b + 1) * period + halo_first, 8, stride=2), :]
-            left = take_lanes(low, left_at)
-            right = jnp.where(
-                kind < 2,
-                jnp.where(kind == 0, take_lanes(low, right_at), take_lanes(high, right_at)),
-                jnp.where(
-                    kind == 2, take_lanes(halo_low, right_at), take_lanes(halo_high, right_at)
-                ),
-            )
-            return left, right
-
+    def by_tile(g, j, of_tile):
         if j == 0:
             return of_tile(0)
         if j == 2:
             return of_tile(1)
         early = lax.broadcasted_iota(jnp.int32, (8, LANES), 1) < LANES // 2
-        left_a, right_a = of_tile(0)
-        left_b, right_b = of_tile(1)
-        return jnp.where(early, left_a, left_b), jnp.where(early, right_a, right_b)
+        return [jnp.where(early, x, y) for x, y in zip(of_tile(0), of_tile(1))]
+
+    def local_sides(g, j, b):
+        here = pl.ds(g * 8, 8)
+        left_at = own_lane[j, here, :]
+        right_at = right_lane[j, here, :]
+        kind = right_kind[j, here, :]
+
+        def of_tile(odd):
+            first = 16 * g + odd
+            low = fields[b, pl.ds(first, 8, stride=2), :]
+            high = fields[b, pl.ds(first + 1, 8, stride=2), :]
+            right = jnp.where(
+                kind == 0,
+                take_lanes(low, right_at),
+                jnp.where(kind == 1, take_lanes(high, right_at), 0.0),
+            )
+            return [take_lanes(low, left_at), right]
+
+        return by_tile(g, j, of_tile)
+
+    def halo_side(g, j, b):
+        here = pl.ds(g * 8, 8)
+        right_at = right_lane[j, here, :]
+        kind = right_kind[j, here, :]
+
+        def of_tile(odd):
+            first = (16 * g) % lists + odd
+            low = halo_rows[pl.ds(2 * b * period + first, 8, stride=2), :]
+            high = halo_rows[pl.ds((2 * b + 1) * period + first, 8, stride=2), :]
+            right = jnp.where(
+                kind == 2,
+                take_lanes(low, right_at),
+                jnp.where(kind == 3, take_lanes(high, right_at), 0.0),
+            )
+            return [right]
+
+        return by_tile(g, j, of_tile)[0]
 
     def put_flux(ref, g, j, b, value):
         for part, piece in enumerate(split(value)):
@@ -339,45 +369,82 @@
             rows, hot, (((1,), (0,)), ((), ())), preferred_element_type=F32
         )
 
-    def scatter(u, odd):
-        result = added(tile_rows(flux_rows, u, odd), signed_hot[2 * u + odd])
-        result = result[:8] + result[8:]
+    def put_cells(u, odd, low, high):
         at = u * 16 + odd * 8
-        cell_rows[0, pl.ds(at, 8), :] = result[:, :LANES]
-        cell_rows[1, pl.ds(at + 8, 8), :] = result[:, LANES:]
-
-    def scatter_size(u, odd):
-        rows = tile_rows(setup_rows, u, odd)
-        at = u * 16 + odd * 8
-        result = added(rows, signed_hot[2 * u + odd])
-        low = lax.broadcasted_iota(jnp.int32, (8, 2 * LANES), 0) < 4
-        summed = result[:8] + jnp.where(low, result[8:], 0.0)
-        cell_rows[0, pl.ds(at, 8), :] = summed[:, :LANES]
-        cell_rows[1, pl.ds(at + 8, 8), :] = summed[:, LANES:]
-        size_cells[0, pl.ds(at, 8), :] = added(rows, plain_hot[2 * u + odd])[8:]
-        size_cells[1, pl.ds(at + 8, 8), :] = -result[8:, LANES:]
-
-    def collect(turn, g, number):
-        def rows(cells_ref, place, first):
-            return cells_ref[place, pl.ds(first, 16, stride=8), :]
-
-        for b in range(min(number, 4)):
+        cell_rows[0, pl.ds(at, 8), :] = low
+        cell_rows[1, pl.ds(at + 8, 8), :] = high
+
+    def scatter(u):
+        for odd in range(2):
+            result = added(tile_rows(flux_rows, u, odd), signed_hot[2 * u + odd])
+            result = result[:8] + result[8:]
+            put_cells(u, odd, result[:, :LANES], result[:, LANES:])
+
+    def own_sums(rows, u):
+        result = added(jnp.concatenate(rows, axis=0), own_hot[u])
+        return [result[16 * odd : 16 * odd + 16, odd * LANES : (odd + 1) * LANES] for odd in range(2)]
+
+    def scatter_halo(u):
+        rows = [tile_rows(flux_rows, u, odd) for odd in range(2)]
+        for odd, result in enumerate(own_sums(rows, u)):
+            own_cells[pl.ds(u * 16 + odd * 8, 8), :] = result[:8] + result[8:]
+
+    def scatter_size(u):
+        rows = [tile_rows(setup_rows, u, odd) for odd in range(2)]
+        own = own_sums(rows, u)
+        for odd in range(2):
+            at = u * 16 + odd * 8
+            result = added(rows[odd], signed_hot[2 * u + odd])
+            low = lax.broadcasted_iota(jnp.int32, (8, 2 * LANES), 0) < 4
+            summed = result[:8] + jnp.where(low, result[8:], 0.0)
+            put_cells(u, odd, summed[:, :LANES], summed[:, LANES:])
+            size_cells[0, pl.ds(at, 8), :] = 2.0 * own[odd][8:] - result[8:, :LANES]
+            size_cells[1, pl.ds(at + 8, 8), :] = -result[8:, LANES:]
+
+    def cell_sums(g, b):
+        def rows(place, first):
+            return cell_rows[place, pl.ds(first, 16, stride=8), :]
+
+        first = 128 * g + b
+        return rows(0, first) + rows(0, first + 4) + (rows(1, first) + rows(1, first + 4))
+
+    def collect_local(g):
+        for b in range(4):
+            local_sums[pl.ds(tiles * b + 16 * g, 16), :] = cell_sums(g, b)
+
+    def collect_halo(turn, g):
+        for b in range(4):
             first = 128 * g + b
-            low = rows(cell_rows, 0, first) + rows(cell_rows, 0, first + 4)
-            high = rows(cell_rows, 1, first) + rows(cell_rows, 1, first + 4)
-            pair_out[turn, pl.ds(tiles * b + 16 * g, 16), :] = low + high
-        if number > 4:
-            pieces = [
-                rows(size_cells, 0, 128 * g + row) + rows(size_cells, 1, 128 * g + row)
-                for row in (4, 5, 6)
-            ]
-            total = pieces[0] + pieces[1] + pieces[2]
-            pair_out[turn, pl.ds(4 * tiles + 16 * g, 16), :] = total
+            here = pl.ds(tiles * b + 16 * g, 16)
+            halo = own_cells[pl.ds(first, 16, stride=8), :]
+            halo = halo + own_cells[pl.ds(first + 4, 16, stride=8), :]
+            pair_out[turn, here, :] = local_sums[here, :] + halo
+        if g == groups - 1:
+            pair_out[turn, pl.ds(4 * tiles, 8), :] = cell_rows[1, pl.ds(8 * tiles, 8), :]
+
+    def collect_setup(g):
+        for b in range(4):
+            local_sums[pl.ds(tiles * b + 16 * g, 16), :] = cell_sums(g, b)
+        pieces = [
+            size_cells[place, pl.ds(128 * g + row, 16, stride=8), :]
+            for place in range(2)
+            for row in (4, 5, 6)
+        ]
+        local_sums[pl.ds(4 * tiles + 16 * g, 16), :] = functools.reduce(jnp.add, pieces)
+
+    def collect_setup_halo(g):
+        for b in range(5):
+            here = pl.ds(tiles * b + 16 * g, 16)
+            total = local_sums[here, :]
+            if b in (0, 4):
+                first = 128 * g + b // 4
+                total = total + own_cells[pl.ds(first, 16, stride=8), :]
+                total = total + own_cells[pl.ds(first + 4, 16, stride=8), :]
+            pair_out[0, here, :] = total
         if g == groups - 1:
             end = pl.ds(8 * tiles, 8)
-            pair_out[turn, pl.ds(number * tiles, 8), :] = cell_rows[1, end, :]
-            if number > 4:
-                pair_out[turn, pl.ds(number * tiles + 8, 8), :] = size_cells[1, end, :]
+            pair_out[0, pl.ds(5 * tiles, 8), :] = cell_rows[1, end, :]
+            pair_out[0, pl.ds(5 * tiles + 8, 8), :] = size_cells[1, end, :]
 
     def wrapped(ref, turn, b):
         number = 5 if turn == 0 else 4
@@ -408,54 +475,79 @@
 
     sent = []
 
-    def flux_steps(g):
+    def coefficients(g, j):
+        here = pl.ds(g * 8, 8)
+        n = [face_n[i, j, here, :] for i in range(3)]
+        return face_u[j, here, :], face_s[j, here, :], n
+
+    def put_fluxes(g, j, u, n, total, jump):
+        for i in range(3):
+            put_flux(flux_rows, g, j, i, u * total[i] + n[i] * total[3] - jump[i])
+        last = n[0] * total[0] + n[1] * total[1] + n[2] * total[2] - jump[3]
+        put_flux(flux_rows, g, j, 3, last)
+
+    def local_steps(g):
         def step(j):
-            here = pl.ds(g * 8, 8)
-            u = face_u[j, here, :]
-            s = face_s[j, here, :]
-            n = [face_n[i, j, here, :] for i in range(3)]
-            both = [sides(g, j, b) for b in range(4)]
+            u, s, n = coefficients(g, j)
+            both = [local_sides(g, j, b) for b in range(4)]
             total = [left + right for left, right in both]
             jump = [s * (right - left) for left, right in both]
-            for i in range(3):
-                put_flux(flux_rows, g, j, i, u * total[i] + n[i] * total[3] - jump[i])
-            last = n[0] * total[0] + n[1] * total[1] + n[2] * total[2] - jump[3]
-            put_flux(flux_rows, g, j, 3, last)
+            put_fluxes(g, j, u, n, total, jump)
 
         return [functools.partial(step, j) for j in range(3)]
 
-    def over_groups(turn, faces, spread, number, search):
-        for stage in range(groups + 2):
+    def halo_steps(g):
+        def step(j):
+            u, s, n = coefficients(g, j)
+            right = [halo_side(g, j, b) for b in range(4)]
+            put_fluxes(g, j, u, n, right, [s * r for r in right])
+
+        return [functools.partial(step, j) for j in range(3)]
+
+    def over_groups(faces, spread, collect, turn=None, number=4):
+        for stage in range(groups + 1 if turn is None else groups + 2):
             queues = []
             if stage < groups:
                 queues.append(faces(stage))
             if 1 <= stage <= groups:
-                queues.append(
-                    [
-                        functools.partial(spread, 8 * (stage - 1) + i, odd)
-                        for i in range(8)
-                        for odd in range(2)
-                    ]
-                )
-            if search and stage >= 2:
+                first = 8 * (stage - 1)
+                queues.append([functools.partial(spread, first + i) for i in range(8)])
+            if turn is not None and stage >= 2:
                 hs = [2 * (stage - 2), 2 * (stage - 2) + 1]
                 if stage == 2:
                     hs = hs[1:]
                 if stage == groups + 1:
                     hs = hs + [0]
-                queues.append(look_up_all(turn, number, hs, stage == 2))
+                queues.append(look_up_all(turn, number, hs, stage == 2, sooner))
             woven(*queues)
             if 1 <= stage <= groups:
-                collect(turn, stage - 1, number)
-        if search:
-            rows = put_listed(turn + 1, [0.0] * number)
-            send_halo(turn + 1, rows, core)
+                collect(stage - 1)
+
+    def sent_sums(turn, number, last=False):
+        fills = [0.0] * number
+        if not last:
+            rows = put_listed(turn + 1, fills, sooner)
+            send_halo(turn + 1, rows, core, sooner)
         copy = pair_copy(turn, number * tiles + 8 * (number - 3))
         sent.append(copy)
+        if not last:
+            for step in look_up_all(turn, number, list(range(tiles // 8)), True, later):
+                step()
+            put_listed(turn + 1, fills, later)
+            send_halo(turn + 1, rows, core, later)
         return copy
 
-    def apply_matrix(turn, values):
-        copy = over_groups(turn, flux_steps, scatter, 4, True)
+    def start_matrix(values):
+        put_field(values)
+        over_groups(local_steps, scatter, collect_local)
+
+    def finish_matrix(turn, halos, last=False):
+        put_halo(halos)
+        collect = functools.partial(collect_halo, turn)
+        over_groups(halo_steps, scatter_halo, collect, None if last else turn)
+        return sent_sums(turn, 4, last)
+
+    def image_of(turn, copy, values):
         sums = pair_sums(turn, copy, 4)
         volume = volume_ref[...]
         return [volume * values[b] + sums[b] for b in range(4)]
@@ -522,6 +614,7 @@
             list_at[at, :] = cell // LANES
             list_col[at, :] = cell - cell // LANES * LANES
     every = list(range(tiles // 8))
+    every_list = list(range(lists))
 
     @pl.when(core == 0)
     def _():
@@ -529,7 +622,7 @@
         for k in range(lists):
             for half in range(halves):
                 look_up(k, half, wanted, every, True)
-        put_listed(0, [0.0] * 3)
+        put_listed(0, [0.0] * 3, every_list)
 
     @pl.when(core == cores - 1)
     def _():
@@ -537,17 +630,17 @@
         for k in range(lists):
             for half in range(halves):
                 look_up(k, half, wanted, every, True)
-        put_listed(turns, [0.0] * 4 + [1.0])
+        put_listed(turns, [0.0] * 4 + [1.0], every_list)
 
     pl.semaphore_wait(barrier, parts * cores - 1)
 
     @pl.when(core == 0)
     def _():
-        send_halo(0, 8, 0)
+        send_halo(0, 8, 0, sooner + later)
 
     @pl.when(core == cores - 1)
     def _():
-        send_halo(turns, 16, 0)
+        send_halo(turns, 16, 0, sooner + later)
 
     lane = lax.broadcasted_iota(jnp.int32, (pairs, LANES), 1)
     pair_id = lax.broadcasted_iota(jnp.int32, (pairs, LANES), 0)
@@ -594,10 +687,9 @@
             at = j * pairs + u
             own = jnp.broadcast_to(own_faces[:, at : at + 1], (LANES, LANES))
             local = jnp.broadcast_to(local_faces[:, at : at + 1], (LANES, LANES))
-            own_hot, local_hot = hot_of(own), hot_of(local)
-            low = own_hot - local_hot
+            own_cell = hot_of(own)
+            low = own_cell - hot_of(local)
             high = -hot_of(local - LANES)
-            plain = own_hot + local_hot
             half = LANES // 2
             if j == 1:
                 places = [(2 * u, LANES, 0, half), (2 * u + 1, LANES, half, LANES)]
@@ -607,7 +699,8 @@
                 rows = slice(row, row + last - first)
                 signed_hot[tile, rows, :LANES] = low[first:last]
                 signed_hot[tile, rows, LANES:] = high[first:last]
-                plain_hot[tile, rows, :] = plain[first:last]
+                lanes = slice(tile % 2 * LANES, (tile % 2 + 1) * LANES)
+                own_hot[u, rows, lanes] = own_cell[first:last]
 
     setup_rows[...] = jnp.zeros_like(setup_rows)
     flux_rows[...] = jnp.zeros_like(flux_rows)
@@ -617,30 +710,47 @@
         copy.wait()
 
     put_field([flow_ref[pl.ds(b, tiles, stride=4), :] for b in range(3)])
-    wait_halo(0)
-    put_halo([[halo_row(0, 0, half * 3 + b) for half in range(halves)] for b in range(3)])
-
     def face_steps(g):
         def step(j):
             here = pl.ds(g * 8, 8)
+            inside = right_kind[j, here, :] < 2
             n = [normal_ref[pl.ds(24 * g + j, 8, stride=3), i, :] for i in range(3)]
-            both = [sides(g, j, b) for b in range(3)]
+            both = [local_sides(g, j, b) for b in range(3)]
             total = [left + right for left, right in both]
-            u = 0.5 * (n[0] * total[0] + n[1] * total[1] + n[2] * total[2])
-            s = jnp.abs(u) + 2.0 * jnp.sqrt(n[0] * n[0] + n[1] * n[1] + n[2] * n[2])
-            u, s = 0.5 * u, 0.5 * s
-            n = [0.5 * n[i] for i in range(3)]
+            u = 0.25 * (n[0] * total[0] + n[1] * total[1] + n[2] * total[2])
+            size = jnp.sqrt(n[0] * n[0] + n[1] * n[1] + n[2] * n[2])
+            face_u[j, here, :] = u
+            face_s[j, here, :] = size
+            put_flux(setup_rows, g, j, 0, jnp.where(inside, u, 0.0))
+            for i in range(3):
+                half = 0.5 * n[i]
+                face_n[i, j, here, :] = half
+                put_flux(setup_rows, g, j, 1 + i, half)
+            put_flux(setup_rows, g, j, 4, jnp.where(inside, jnp.abs(u) + size, 0.0))
+
+        return [functools.partial(step, j) for j in range(3)]
+
+    def face_halo_steps(g):
+        def step(j):
+            here = pl.ds(g * 8, 8)
+            outside = right_kind[j, here, :] >= 2
+            u, size, n = coefficients(g, j)
+            right = [halo_side(g, j, b) for b in range(3)]
+            u = u + 0.5 * (n[0] * right[0] + n[1] * right[1] + n[2] * right[2])
+            s = jnp.abs(u) + size
             face_u[j, here, :] = u
             face_s[j, here, :] = s
-            put_flux(setup_rows, g, j, 0, u)
-            for i in range(3):
-                face_n[i, j, here, :] = n[i]
-                put_flux(setup_rows, g, j, 1 + i, n[i])
-            put_flux(setup_rows, g, j, 4, s)
+            put_flux(flux_rows, g, j, 0, jnp.where(outside, u, 0.0))
+            put_flux(flux_rows, g, j, 1, jnp.where(outside, s, 0.0))
 
         return [functools.partial(step, j) for j in range(3)]
 
-    copy = over_groups(0, face_steps, scatter_size, 5, True)
+    over_groups(face_steps, scatter_size, collect_setup)
+    wait_halo(0)
+    put_halo([[halo_row(0, 0, half * 3 + b) for half in range(halves)] for b in range(3)])
+
+    over_groups(face_halo_steps, scatter_halo, collect_setup_halo, 0, 5)
+    copy = sent_sums(0, 5)
     rvd, rschur, coupling = inverse(volume_ref[...], pair_sums(0, copy, 5))
     blocks[0] = rvd
     blocks[1] = rschur
@@ -649,7 +759,7 @@
 
     shadow = load_source()
     pre = precondition(shadow)
-    put_field(pre)
+    start_matrix(pre)
     wait_halo(turns)
 
     def first_halo(b):
@@ -663,20 +773,20 @@
         inverse(halo_volume[half], [sums[b][half] for b in range(5)]) for half in range(halves)
     ]
     halo_pre = precondition_halo(halo_residual)
-    put_halo(halo_pre)
 
     V, T, W, MIDDLE, SECOND, SUM = range(6)
-    image = apply_matrix(1, pre)
+    copy = finish_matrix(1, halo_pre)
+    image = image_of(1, copy, pre)
     shadow = load_source()
     start_dots(0, [dot(shadow, shadow), dot(shadow, image)])
     save(V, image)
     pre = precondition(image)
-    put_field(pre)
+    start_matrix(pre)
     halo_v = halo_image(2, halo_pre)
     halo_pre = precondition_halo(halo_v)
-    put_halo(halo_pre)
-
-    twice = apply_matrix(2, pre)
+
+    copy = finish_matrix(2, halo_pre)
+    twice = image_of(2, copy, pre)
     rho, shadow_image = wait_dots(0, 2)
     alpha = rho / shadow_image
     shadow, image = load_source(), load(V)
@@ -689,12 +799,12 @@
     save(MIDDLE, middle)
     save(SECOND, second)
     pre = precondition(twice)
-    put_field(pre)
+    start_matrix(pre)
     halo_t = halo_image(3, halo_pre)
     halo_pre = precondition_halo(halo_t)
-    put_halo(halo_pre)
-
-    thrice = apply_matrix(3, pre)
+
+    copy = finish_matrix(3, halo_pre)
+    thrice = image_of(3, copy, pre)
     second_mid, second_sq, shadow_mid, shadow_second = wait_dots(1, 4)
     omega = second_mid / second_sq
     rho_next = shadow_mid - omega * shadow_second
@@ -717,7 +827,7 @@
     save(SUM, combine([alpha * x for x in shadow], omega, middle))
     save(MIDDLE, direction)
     pre = precondition(next_image)
-    put_field(pre)
+    start_matrix(pre)
     halo_w = halo_image(4, halo_pre)
     halo_second = combine_halo(halo_v, -alpha, halo_t)
     halo_next = combine_halo(
@@ -725,9 +835,7 @@
         beta,
         combine_halo(halo_v, -omega, halo_t),
     )
-    put_halo(precondition_halo(halo_next))
-
-    copy = over_groups(4, flux_steps, scatter, 4, False)
+    copy = finish_matrix(4, precondition_halo(halo_next), last=True)
     (shadow_image,) = wait_dots(2, 1)
     alpha = rho_next / shadow_image
     middle = combine(load(T), -alpha, load(V))
@@ -797,7 +905,7 @@
     ints = pltpu.VMEM((3, pairs, LANES), jnp.int32)
     floats = pltpu.VMEM((3, pairs, LANES), F32)
     hot = pltpu.VMEM((tiles, 3 * LANES // 2, 2 * LANES), BF16)
-    out = jax.ShapeDtypeStruct((4 * tiles, LANES), F32)
+    out = pltpu.VMEM((4 * tiles, LANES), F32)
     solved, left = pl.pallas_call(
         functools.partial(kernel, parts, cores),
         out_shape=(out, out),
@@ -826,11 +934,13 @@
             floats,
             pltpu.VMEM((3, 3, pairs, LANES), F32),
             hot,
-            pltpu.VMEM((tiles, 3 * LANES // 2, LANES), BF16),
+            pltpu.VMEM((pairs, 3 * LANES // 2, 2 * LANES), BF16),
             pltpu.VMEM((3, 16 * pairs, LANES), F32),
             pltpu.VMEM((3, 16 * pairs, LANES), F32),
             pltpu.VMEM((2, 8 * tiles + 8, LANES), F32),
             pltpu.VMEM((2, 8 * tiles + 8, LANES), F32),
+            pltpu.VMEM((8 * tiles, LANES), F32),
+            pltpu.VMEM((5 * tiles, LANES), F32),
             pltpu.VMEM((4, tiles + 8, LANES), F32),
             pltpu.VMEM((8 * period, LANES), F32),
             pltpu.VMEM((8 * lists, LANES), F32),

time: 48.1 us -> 43.2 us (0.90)
  Pallas kernels: 44.4 us -> 40.4 us
  local copies, waits for them, and re-layouts: 2.26 us -> 1.31 us
    pallas_call x1, Pallas kernels: 44.4 us -> 40.4 us  [body(): pl.pallas_call(functools.partial(kernel, parts, cores), out_shape=(out, o...]
    unnamed x4 -> x2, local copies, waits for them, and re-layouts: 2.26 us -> 1.31 us
where the time goes in v3:
time: 43.2 us; the launch traced here: 43 us
  Pallas kernels  40.4 us (94%)
  local copies, waits for them, and re-layouts  1.31 us (3%)
  between operations  1.29 us (3%)
    pallas_call x1, Pallas kernels, body(): pl.pallas_call(functools.partial(kernel, parts, cores), out_shape=(out, o...  40.4 us
    unnamed x2, local copies, waits for them, and re-layouts  1.31 us

profile of v3, /device:TPU:0, one launch (start us, length us, event | category | flops | bytes accessed | tf_op | source)
XLA Modules:
  0.0 43.0 jit_solution(1814232831868857343)
XLA Ops:
  1.3 40.4 %shard_map.104 = (f32[256,128]{1,0:T(8,128)S(1)}, f32[256,128]{1,0:T(8,128)S(1)}) custom-call(s32[1]{0:T(128)S(6)} %copy.19.count_hbm, f32[256,128]{1,0:T(8,128)} %bitcast.29, f32[256,128]{1,0:T(8,128)} %bitcast.30, f32[64,128]{1,0:T(8,128)} %bitcast.33, f32[96,3,128]{2,1,0:T(4,128)} %bitcast.28, s32[96,128]{1,0:T(8,128)} %bitcast.31, s32[96,128]{1,0:T(8,128)} %bitcast.32, ...), custom_call_target="tpu_custom_call" | custom-call | tf_op jit(solution)/shard_map/pallas_call | solution.py:909
  41.7 0.7 %copy.17 = f32[4,8192]{1,0:T(4,128)} copy(f32[4,8192]{1,0:T(4,128)S(1)} %bitcast.27) | data formatting | bytes 262144
  42.3 0.7 %copy.18 = f32[4,8192]{1,0:T(4,128)} copy(f32[4,8192]{1,0:T(4,128)S(1)} %bitcast.26) | data formatting | bytes 262144

commit v4 on v3

--- a/solution.py
+++ b/solution.py
@@ -43,8 +43,7 @@
     neighbour_hbm,
     list_hbm,
     halo_count_hbm,
-    solution_ref,
-    residual_ref,
+    out_ref,
     flow_ref,
     source_ref,
     volume_ref,
@@ -76,7 +75,6 @@
     local_sums,
     fields,
     halo_rows,
-    halo_mix,
     blocks,
     vecs,
     pair_out,
@@ -301,10 +299,8 @@
     def put_halo(values):
         for b, value in enumerate(values):
             for half in range(halves):
-                halo_mix[pl.ds(halves * b + half, lists, stride=8), :] = value[half]
-        for t in range(period):
-            mixed = halo_mix[pl.ds(8 * (t % lists), 8), :]
-            halo_rows[pl.ds(t, 8, stride=period), :] = mixed
+                rows = jnp.concatenate([value[half]] * (-(-period // lists)), axis=0)
+                halo_rows[pl.ds((halves * b + half) * period, period), :] = rows[:period]
 
     def by_tile(g, j, of_tile):
         if j == 0:
@@ -354,15 +350,17 @@
     def put_flux(ref, g, j, b, value):
         for part, piece in enumerate(split(value)):
             row = 4 * part + b if b < 4 else 12 + part
-            ref[j, pl.ds(128 * g + row, 8, stride=16), :] = piece
+            ref[row // 8, j, pl.ds(64 * g + row % 8, 8, stride=8), :] = piece
 
     def tile_rows(rows_ref, u, odd):
-        at = pl.ds(u * 16, 16)
-        middle = rows_ref[1, at, :]
-        if odd:
-            middle = pltpu.roll(middle, LANES // 2, 1)
-        rows = jnp.concatenate([rows_ref[2 * odd, at, :], middle], axis=1)
-        return rows[:, : 3 * LANES // 2].astype(BF16)
+        at = pl.ds(u * 8, 8)
+        pieces = []
+        for half in range(2):
+            middle = rows_ref[half, 1, at, :]
+            if odd:
+                middle = pltpu.roll(middle, LANES // 2, 1)
+            pieces.append(jnp.concatenate([rows_ref[half, 2 * odd, at, :], middle], axis=1))
+        return jnp.concatenate(pieces, axis=0)[:, : 3 * LANES // 2].astype(BF16)
 
     def added(rows, hot):
         return lax.dot_general(
@@ -849,8 +847,8 @@
     second_mid, second_sq = wait_dots(3, 2)
     omega = second_mid / second_sq
     for b in range(4):
-        solution_ref[pl.ds(b, tiles, stride=4), :] = known[b] + omega * pre_mid[b]
-        residual_ref[pl.ds(b, tiles, stride=4), :] = middle[b] - omega * second[b]
+        out_ref[pl.ds(b, tiles, stride=4), :] = known[b] + omega * pre_mid[b]
+        out_ref[pl.ds(4 * tiles + b, tiles, stride=4), :] = middle[b] - omega * second[b]
 
     @pl.when(core == 0)
     def _():
@@ -905,12 +903,11 @@
     ints = pltpu.VMEM((3, pairs, LANES), jnp.int32)
     floats = pltpu.VMEM((3, pairs, LANES), F32)
     hot = pltpu.VMEM((tiles, 3 * LANES // 2, 2 * LANES), BF16)
-    out = pltpu.VMEM((4 * tiles, LANES), F32)
-    solved, left = pl.pallas_call(
+    both = pl.pallas_call(
         functools.partial(kernel, parts, cores),
-        out_shape=(out, out),
+        out_shape=pltpu.VMEM((8 * tiles, LANES), F32),
         in_specs=[hbm] * 9,
-        out_specs=(vmem, vmem),
+        out_specs=vmem,
         scratch_shapes=[
             pltpu.VMEM((4 * tiles, LANES), F32),
             pltpu.VMEM((4 * tiles, LANES), F32),
@@ -935,15 +932,14 @@
             pltpu.VMEM((3, 3, pairs, LANES), F32),
             hot,
             pltpu.VMEM((pairs, 3 * LANES // 2, 2 * LANES), BF16),
-            pltpu.VMEM((3, 16 * pairs, LANES), F32),
-            pltpu.VMEM((3, 16 * pairs, LANES), F32),
+            pltpu.VMEM((2, 3, 8 * pairs, LANES), F32),
+            pltpu.VMEM((2, 3, 8 * pairs, LANES), F32),
             pltpu.VMEM((2, 8 * tiles + 8, LANES), F32),
             pltpu.VMEM((2, 8 * tiles + 8, LANES), F32),
             pltpu.VMEM((8 * tiles, LANES), F32),
             pltpu.VMEM((5 * tiles, LANES), F32),
             pltpu.VMEM((4, tiles + 8, LANES), F32),
             pltpu.VMEM((8 * period, LANES), F32),
-            pltpu.VMEM((8 * lists, LANES), F32),
             pltpu.VMEM((5, tiles, LANES), F32),
             pltpu.VMEM((6, 4, tiles, LANES), F32),
             pltpu.VMEM((turns, 5 * tiles + 16, LANES), F32),
@@ -973,7 +969,7 @@
         send_list,
         halo_count,
     )
-    return by_component(solved), by_component(left)
+    return by_component(both[: 4 * tiles]), by_component(both[4 * tiles :])
 
 
 def solution(mesh):

time: 43.2 us -> 42.3 us (0.979)
  local copies, waits for them, and re-layouts: 1.31 us -> 0.72 us
    unnamed x2 -> x0, local copies, waits for them, and re-layouts: 1.31 us -> none
    slice x0 -> x1, local copies, waits for them, and re-layouts: none -> 0.72 us  [body(): return (by_component(both[:4 * tiles]), by_component(both[4 * tiles:]))]
where the time goes in v4:
time: 42.3 us; the launch traced here: 42.2 us
  Pallas kernels  40.2 us (95%)
  between operations  1.29 us (3%)
  local copies, waits for them, and re-layouts  0.72 us (2%)
    pallas_call x1, Pallas kernels, body(): pl.pallas_call(functools.partial(kernel, parts, cores), out_shape=pltpu.V...  40.2 us

profile of v4, /device:TPU:0, one launch (start us, length us, event | category | flops | bytes accessed | tf_op | source)
XLA Modules:
  0.0 42.2 jit_solution(3627557770013392381)
XLA Ops:
  1.3 40.2 %shard_map.104 = f32[512,128]{1,0:T(8,128)S(1)} custom-call(s32[1]{0:T(128)S(6)} %copy.15.count_hbm, f32[256,128]{1,0:T(8,128)} %bitcast.27, f32[256,128]{1,0:T(8,128)} %bitcast.28, f32[64,128]{1,0:T(8,128)} %bitcast.33, f32[96,3,128]{2,1,0:T(4,128)} %bitcast.26, s32[96,128]{1,0:T(8,128)} %bitcast.31, s32[96,128]{1,0:T(8,128)} %bitcast.32, ...), custom_call_target="tpu_custom_call" | custom-call | tf_op jit(solution)/shard_map/pallas_call | solution.py:906
  41.5 0.7 %fusion = (f32[256,128]{1,0:T(8,128)}, f32[256,128]{1,0:T(8,128)}) fusion(f32[512,128]{1,0:T(8,128)S(1)} %shard_map.104), kind=kLoop, calls=%fused_computation | loop fusion | bytes 524288 | tf_op jit(solution)/shard_map/slice | solution.py:972

commit v5 on v4

--- a/solution.py
+++ b/solution.py
@@ -409,6 +409,16 @@
     def collect_local(g):
         for b in range(4):
             local_sums[pl.ds(tiles * b + 16 * g, 16), :] = cell_sums(g, b)
+        if g == groups - 1:
+            add_wraps(4)
+
+    def add_wraps(number):
+        for b in range(number):
+            ref, places = (cell_rows, (b, b + 4)) if b < 4 else (size_cells, (4, 5, 6))
+            wrap = [ref[1, pl.ds(8 * tiles + place, 1), :] for place in places]
+            here = pl.ds(tiles * b, 8)
+            wrap = jnp.where(row8 == 0, functools.reduce(jnp.add, wrap), 0.0)
+            local_sums[here, :] = local_sums[here, :] + wrap
 
     def collect_halo(turn, g):
         for b in range(4):
@@ -417,8 +427,6 @@
             halo = own_cells[pl.ds(first, 16, stride=8), :]
             halo = halo + own_cells[pl.ds(first + 4, 16, stride=8), :]
             pair_out[turn, here, :] = local_sums[here, :] + halo
-        if g == groups - 1:
-            pair_out[turn, pl.ds(4 * tiles, 8), :] = cell_rows[1, pl.ds(8 * tiles, 8), :]
 
     def collect_setup(g):
         for b in range(4):
@@ -429,6 +437,8 @@
             for row in (4, 5, 6)
         ]
         local_sums[pl.ds(4 * tiles + 16 * g, 16), :] = functools.reduce(jnp.add, pieces)
+        if g == groups - 1:
+            add_wraps(5)
 
     def collect_setup_halo(g):
         for b in range(5):
@@ -439,37 +449,14 @@
                 total = total + own_cells[pl.ds(first, 16, stride=8), :]
                 total = total + own_cells[pl.ds(first + 4, 16, stride=8), :]
             pair_out[0, here, :] = total
-        if g == groups - 1:
-            end = pl.ds(8 * tiles, 8)
-            pair_out[0, pl.ds(5 * tiles, 8), :] = cell_rows[1, end, :]
-            pair_out[0, pl.ds(5 * tiles + 8, 8), :] = size_cells[1, end, :]
-
-    def wrapped(ref, turn, b):
-        number = 5 if turn == 0 else 4
-
-        def row(at):
-            return ref[turn, pl.ds(number * tiles + at, 1), :]
-
-        if b < 4:
-            return row(b) + row(b + 4)
-        return row(12) + row(13) + row(14)
 
     def partial_field(turn, b, h):
-        found = pair_out[turn, pl.ds(tiles * b + 8 * h, 8), :]
-        if h == 0:
-            found = found + jnp.where(row8 == 0, wrapped(pair_out, turn, b), 0.0)
-        return found
+        return pair_out[turn, pl.ds(tiles * b + 8 * h, 8), :]
 
     def pair_sums(turn, copy, number):
         copy.wait_recv()
-        first = lax.broadcasted_iota(jnp.int32, (tiles, LANES), 0) == 0
-        sums = []
-        for b in range(number):
-            rows = pl.ds(tiles * b, tiles)
-            wrap = wrapped(pair_out, turn, b) + wrapped(pair_in, turn, b)
-            total = pair_out[turn, rows, :] + pair_in[turn, rows, :]
-            sums.append(total + jnp.where(first, wrap, 0.0))
-        return sums
+        parts_of = [pl.ds(tiles * b, tiles) for b in range(number)]
+        return [pair_out[turn, rows, :] + pair_in[turn, rows, :] for rows in parts_of]
 
     sent = []
 
@@ -512,10 +499,6 @@
                 queues.append([functools.partial(spread, first + i) for i in range(8)])
             if turn is not None and stage >= 2:
                 hs = [2 * (stage - 2), 2 * (stage - 2) + 1]
-                if stage == 2:
-                    hs = hs[1:]
-                if stage == groups + 1:
-                    hs = hs + [0]
                 queues.append(look_up_all(turn, number, hs, stage == 2, sooner))
             woven(*queues)
             if 1 <= stage <= groups:
@@ -526,7 +509,7 @@
         if not last:
             rows = put_listed(turn + 1, fills, sooner)
             send_halo(turn + 1, rows, core, sooner)
-        copy = pair_copy(turn, number * tiles + 8 * (number - 3))
+        copy = pair_copy(turn, number * tiles)
         sent.append(copy)
         if not last:
             for step in look_up_all(turn, number, list(range(tiles // 8)), True, later):
@@ -942,8 +925,8 @@
             pltpu.VMEM((8 * period, LANES), F32),
             pltpu.VMEM((5, tiles, LANES), F32),
             pltpu.VMEM((6, 4, tiles, LANES), F32),
-            pltpu.VMEM((turns, 5 * tiles + 16, LANES), F32),
-            pltpu.VMEM((turns, 5 * tiles + 16, LANES), F32),
+            pltpu.VMEM((turns, 5 * tiles, LANES), F32),
+            pltpu.VMEM((turns, 5 * tiles, LANES), F32),
             pltpu.VMEM((turns + 1, lists, 16, LANES), F32),
             pltpu.VMEM((turns + 1, cores, 16 * lists, LANES), F32),
             pltpu.VMEM((turns + 8, 1, LANES), F32),

time: 42.3 us -> 42.3 us (level)
  no operation moved by 1% of the time
where the time goes in v5:
time: 42.3 us; the launch traced here: 42.1 us
  Pallas kernels  40.1 us (95%)
  between operations  1.29 us (3%)
  local copies, waits for them, and re-layouts  0.72 us (2%)
    pallas_call x1, Pallas kernels, body(): pl.pallas_call(functools.partial(kernel, parts, cores), out_shape=pltpu.V...  40.1 us

profile of v5, /device:TPU:0, one launch (start us, length us, event | category | flops | bytes accessed | tf_op | source)
XLA Modules:
  0.0 42.1 jit_solution(16691800361133830628)
XLA Ops:
  1.3 40.1 %shard_map.104 = f32[512,128]{1,0:T(8,128)S(1)} custom-call(s32[1]{0:T(128)S(6)} %copy.15.count_hbm, f32[256,128]{1,0:T(8,128)} %bitcast.27, f32[256,128]{1,0:T(8,128)} %bitcast.28, f32[64,128]{1,0:T(8,128)} %bitcast.33, f32[96,3,128]{2,1,0:T(4,128)} %bitcast.26, s32[96,128]{1,0:T(8,128)} %bitcast.31, s32[96,128]{1,0:T(8,128)} %bitcast.32, ...), custom_call_target="tpu_custom_call" | custom-call | tf_op jit(solution)/shard_map/pallas_call | solution.py:889
  41.4 0.7 %fusion = (f32[256,128]{1,0:T(8,128)}, f32[256,128]{1,0:T(8,128)}) fusion(f32[512,128]{1,0:T(8,128)S(1)} %shard_map.104), kind=kLoop, calls=%fused_computation | loop fusion | bytes 524288 | tf_op jit(solution)/shard_map/slice | solution.py:955
